TPU v7x, 256 devices: a whole 4x4x8 slice. The times are simulated.
256 devices in a mesh: slab: 128 (over z, y, x), sub: 2 (over core).
Axes of the slice: x: 4, y: 4, z: 8, core: 2. Of those that a mesh axis runs over, the one named last changes fastest.
Arguments:
- start: float32 [4, 768, 32, 256], P(None, 'slab', 'sub'), may hold values from -6 to 6
- wind: float32 [3, 768, 32, 256], P(None, 'slab', 'sub'), may hold values from -4 to 4
- reaction: float32 [768, 32, 256], P('slab', 'sub'), may hold values from 0.5 to 4
- mass: float32 [768, 32, 256], P('slab', 'sub'), may hold values from 0.5 to 2
Outputs:
- basis: float32 [4, 4, 768, 32, 256], P(None, None, 'slab', 'sub')
- search: float32 [3, 4, 768, 32, 256], P(None, None, 'slab', 'sub')
- hessenberg: float32 [4, 3], replicated
All inputs are finite; a program needn't handle non-finite values.
Results may differ from a plain program's by a relative error of at most 0.0003.
Values sent between devices are 32-bit elements; how exact they have to be, the bound alone decides.
A program may use at most 64 MiB of HBM per device.

v0:
```python
import functools

import jax
import jax.numpy as jnp
from jax import lax
from jax.sharding import Mesh
from jax.sharding import PartitionSpec as P

ITERS = 3
SLAB = ("slab_0", "slab_1", "slab_2")
SLAB_SUB = ("slab_0", "slab_1", "slab_2", "sub")


def padded_2(shard, sides, width):
    for axis, dim in sides:
        devices, length = (lax.axis_size(axis), shard.shape[dim])
        up = [(i, (i + 1) % devices) for i in range(devices - 1)]
        down = [(j, i) for i, j in up]
        last = lax.slice_in_dim(shard, length - width, length, axis=dim)
        leading = lax.slice_in_dim(shard, 0, width, axis=dim)
        before = lax.ppermute(last, axis, up)
        after = lax.ppermute(leading, axis, down)
        shard = jnp.concatenate([before, shard, after], axis=dim)
    return shard


def over_axes(shard, axes):
    return functools.reduce(lax.psum, axes, shard)


def neighbour_sets(padded):
    center = padded[..., 1:-1, 1:-1, :]
    zero_face = jnp.zeros_like(center[..., :1])
    plus_side = (
        padded[..., 2:, 1:-1, :],
        padded[..., 1:-1, 2:, :],
        jnp.concatenate([center[..., 1:], zero_face], -1),
    )
    minus_side = (
        padded[..., :-2, 1:-1, :],
        padded[..., 1:-1, :-2, :],
        jnp.concatenate([zero_face, center[..., :-1]], -1),
    )
    return (center, plus_side, minus_side)


def six_sum(plus_side, minus_side):
    total = plus_side[0] + minus_side[0]
    total = total + plus_side[1] + minus_side[1]
    return total + plus_side[2] + minus_side[2]


def transport(padded, reaction_k, wind_k):
    center, plus_side, minus_side = neighbour_sets(padded)
    convect = wind_k[0] * (plus_side[0] - minus_side[0])
    convect = convect + wind_k[1] * (plus_side[1] - minus_side[1])
    convect = convect + wind_k[2] * (plus_side[2] - minus_side[2])
    return (6.0 + reaction_k) * center - six_sum(plus_side, minus_side) + 0.5 * convect


def gradient(padded):
    center, plus_side, minus_side = neighbour_sets(padded)
    return jnp.stack(
        [0.5 * (plus_side[dim_index] - minus_side[dim_index]) for dim_index in range(3)]
    )


def divergence(padded):
    center, plus_side, minus_side = neighbour_sets(padded)
    total = 0.5 * (plus_side[0][0] - minus_side[0][0])
    total = total + 0.5 * (plus_side[1][1] - minus_side[1][1])
    return total + 0.5 * (plus_side[2][2] - minus_side[2][2])


def pressure_poisson(padded):
    center, plus_side, minus_side = neighbour_sets(padded)
    return 7.0 * center - six_sum(plus_side, minus_side)


def oseen_apply(padded, reaction_k, wind_k):
    upper = transport(padded[:3], reaction_k, wind_k) + gradient(padded[3])
    center, plus_side, minus_side = neighbour_sets(padded[3])
    lower = -divergence(padded[:3]) - 0.5 * (6.0 * center - six_sum(plus_side, minus_side))
    return jnp.concatenate([upper, lower[None]], 0)


def local_dots(vectors, image):
    return jnp.stack([jnp.sum(vector * image) for vector in vectors])


def combine_back(raw, projected, held, norm_next):
    result = raw
    for row in range(len(held)):
        result = result - projected[row] * held[row]
    return result / norm_next


def per_device(start, wind, reaction, mass):
    cells_x = start.shape[1]
    cells_y = start.shape[2]

    def inside(width):
        global_x = (
            lax.axis_index(SLAB) * cells_x
            - width
            + jnp.arange(cells_x + 2 * width, dtype=jnp.int32)
        )
        global_y = (
            lax.axis_index("sub") * cells_y
            - width
            + jnp.arange(cells_y + 2 * width, dtype=jnp.int32)
        )
        inside_x = (global_x >= 0) & (global_x < cells_x * lax.axis_size(SLAB))
        inside_y = (global_y >= 0) & (global_y < cells_y * lax.axis_size("sub"))
        return (inside_x[:, None] & inside_y[None, :])[:, :, None]

    stacked = jnp.concatenate([wind, reaction[None], mass[None]], 0)
    coeffs = padded_2(stacked, ((SLAB, 1), ("sub", 2)), 3)

    def coef_at(width):
        offset = 3 - width
        return coeffs[
            :, offset : offset + cells_x + 2 * width, offset : offset + cells_y + 2 * width, :
        ]

    def apply_both(vector):
        extended = padded_2(vector, ((SLAB, 1), ("sub", 2)), 5)
        pressure = extended[3]
        first_guess = pressure / 7.0
        second_guess = (
            first_guess[1:-1, 1:-1] + (pressure[1:-1, 1:-1] - pressure_poisson(first_guess)) / 7.0
        )
        second_guess = jnp.where(inside(4), second_guess, 0.0)
        coef_three = coef_at(3)
        schur = jnp.where(
            inside(3), -transport(second_guess, coef_three[3], coef_three[:3]) / coef_three[4], 0.0
        )
        residue = jnp.where(inside(2), extended[:3, 3:-3, 3:-3] - gradient(schur), 0.0)
        coef_two = coef_at(2)
        velocity_first = residue / (6.0 + coef_two[3])
        coef_one = coef_at(1)
        velocity = velocity_first[:, 1:-1, 1:-1] + (
            residue[:, 1:-1, 1:-1] - transport(velocity_first, coef_one[3], coef_one[:3])
        ) / (6.0 + coef_one[3])
        velocity = jnp.where(inside(1), velocity, 0.0)
        found = jnp.concatenate([velocity, schur[None, 2:-2, 2:-2]], 0)
        image = oseen_apply(found, reaction, wind)
        return (found[:, 1:-1, 1:-1], image)

    scale_start = jnp.sqrt(over_axes(jnp.sum(start * start), SLAB_SUB))
    vectors = [start / scale_start]
    first_found, first_image = apply_both(vectors[0])
    searches = [first_found]
    images = [first_image]
    hess = jnp.zeros((ITERS + 1, ITERS), jnp.float32)
    for column in range(ITERS):
        image = images[column]
        raw_image = image
        ahead = None
        if column + 1 < ITERS:
            ahead = apply_both(raw_image)
        projected, squared = (
            over_axes(local_dots(vectors, image), SLAB_SUB),
            over_axes(jnp.sum(image * image), SLAB_SUB),
        )
        for row in range(column + 1):
            image = image - projected[row] * vectors[row]
        norm_next = jnp.sqrt(squared - jnp.sum(projected * projected))
        hess = hess.at[: column + 1, column].set(projected)
        hess = hess.at[column + 1, column].set(norm_next)
        vectors.append(image / norm_next)
        if column + 1 < ITERS:
            next_found = combine_back(ahead[0], projected, searches, norm_next)
            next_image = combine_back(ahead[1], projected, images, norm_next)
            searches.append(next_found)
            images.append(next_image)
    return (jnp.stack(vectors), jnp.stack(searches), hess)


def solution(mesh):
    finer = Mesh(
        mesh.devices.reshape(8, 4, 4, mesh.shape["sub"]), ("slab_0", "slab_1", "slab_2", "sub")
    )
    in_specs = (
        P(None, SLAB, "sub", None),
        P(None, SLAB, "sub", None),
        P(SLAB, "sub", None),
        P(SLAB, "sub", None),
    )
    out_specs = (P(None, None, SLAB, "sub", None), P(None, None, SLAB, "sub", None), P())
    return jax.shard_map(
        per_device, mesh=finer, in_specs=in_specs, out_specs=out_specs, check_vma=False
    )
```

profile of v0, /device:TPU:1, one launch (start us, length us, event | category | flops | bytes accessed | tf_op | source)
XLA Modules:
  0.0 305.2 jit_solution(3049331386067701832)
XLA Ops:
  0.7 1.8 multiply_reduce_fusion.9
  2.4 17.9 %psum.196 = f32[]{:T(128)} all-reduce(f32[]{:T(128)} %multiply_reduce_fusion.9), channel_id=1, replica_groups=mesh['slab_0'=8,'slab_1'=4,'slab_2'=4,'sub'=2] {'slab_0'}, use_global_device_ids=true, to_apply=%region_1.0 | all-reduce | flops 1 | bytes 8 | tf_op jit(solution)/shard_map/psum | solution.py:28
  20.3 9.3 %psum.197 = f32[]{:T(128)} all-reduce(f32[]{:T(128)} %psum.196), channel_id=1, replica_groups=mesh['slab_0'=8,'slab_1'=4,'slab_2'=4,'sub'=2] {'slab_1'}, use_global_device_ids=true, to_apply=%region_2.0 | all-reduce | flops 1 | bytes 8 | tf_op jit(solution)/shard_map/psum | solution.py:28
  29.7 9.3 %psum.198 = f32[]{:T(128)} all-reduce(f32[]{:T(128)} %psum.197), channel_id=1, replica_groups=mesh['slab_0'=8,'slab_1'=4,'slab_2'=4,'sub'=2] {'slab_2'}, use_global_device_ids=true, to_apply=%region_3.0 | all-reduce | flops 1 | bytes 8 | tf_op jit(solution)/shard_map/psum | solution.py:28
  39.0 10.8 %psum.199 = f32[]{:T(128)} all-reduce(f32[]{:T(128)} %psum.198), channel_id=1, replica_groups=mesh['slab_0'=8,'slab_1'=4,'slab_2'=4,'sub'=2] {'sub'}, use_global_device_ids=true, to_apply=%region_4.0 | all-reduce | flops 1 | bytes 8 | tf_op jit(solution)/shard_map/psum | solution.py:28
  50.4 1.0 broadcast_divide_fusion.3
  51.5 1.3 collective-permute-start.1
  52.8 4.0 %collective-permute-start = (f32[4,5,16,256]{3,2,1,0:T(8,128)S(1)}, f32[4,5,16,256]{3,2,1,0:T(8,128)S(1)}, u32[]{:S(2)}, u32[]{:S(2)}) collective-permute-start(f32[4,5,16,256]{3,2,1,0:T(8,128)S(1)} %get-tuple-element.166), channel_id=1, source_target_pairs={{0,2},{2,4},{4,6},{6,8},{8,10},{10,12},{12,14},{14,16},{16,18},{18... | collective-permute-start | bytes 983048 | tf_op jit(solution)/shard_map/ppermute | solution.py:21
  57.0 1.3 collective-permute-start.5
  58.3 4.0 %collective-permute-start.4 = (f32[5,3,16,256]{3,2,1,0:T(8,128)S(1)}, f32[5,3,16,256]{3,2,1,0:T(8,128)S(1)}, u32[]{:S(2)}, u32[]{:S(2)}) collective-permute-start(f32[5,3,16,256]{3,2,1,0:T(8,128)S(1)} %get-tuple-element.160), channel_id=1, source_target_pairs={{0,2},{2,4},{4,6},{6,8},{8,10},{10,12},{12,14},{14,16},{16,18},{18... | collective-permute-start | bytes 737288 | tf_op jit(solution)/shard_map/ppermute | solution.py:21
  64.8 2.8 collective-permute-done.5
  67.6 0.9 collective-permute-done.4
  68.6 3.4 %collective-permute-start.7 = (f32[5,12,3,256]{3,2,1,0:T(4,128)S(1)}, f32[5,12,3,256]{3,2,1,0:T(4,128)S(1)}, u32[]{:S(2)}, u32[]{:S(2)}) collective-permute-start(f32[5,12,3,256]{3,2,1,0:T(4,128)S(1)} %get-tuple-element.140), channel_id=1, source_target_pairs={{1,0},{3,2},{5,4},{7,6},{9,8},{11,10},{13,12},{15,14},{17,16},{19,... | collective-permute-start | bytes 552968 | tf_op jit(solution)/shard_map/ppermute | solution.py:22
  72.0 1.3 collective-permute-start.6
  73.5 3.1 %collective-permute-start.3 = (f32[4,16,5,256]{3,2,1,0:T(8,128)S(1)}, f32[4,16,5,256]{3,2,1,0:T(8,128)S(1)}, u32[]{:S(2)}, u32[]{:S(2)}) collective-permute-start(f32[4,16,5,256]{3,2,1,0:T(8,128)S(1)} %get-tuple-element.138), channel_id=1, source_target_pairs={{1,0},{3,2},{5,4},{7,6},{9,8},{11,10},{13,12},{15,14},{17,16},{19,... | collective-permute-start | bytes 983048 | tf_op jit(solution)/shard_map/ppermute | solution.py:22
  76.6 1.3 collective-permute-start.2
  77.9 1.2 pad_maximum_fusion.1
  79.3 1.1 collective-permute-done.2
  83.9 1.3 collective-permute-start.9
  85.2 4.8 %collective-permute-start.8 = (f32[4,5,16,256]{3,2,1,0:T(8,128)S(1)}, f32[4,5,16,256]{3,2,1,0:T(8,128)S(1)}, u32[]{:S(2)}, u32[]{:S(2)}) collective-permute-start(f32[4,5,16,256]{3,2,1,0:T(8,128)S(1)} %get-tuple-element.164), channel_id=1, source_target_pairs={{0,2},{2,4},{4,6},{6,8},{8,10},{10,12},{12,14},{14,16},{16,18},{18... | collective-permute-start | bytes 983048 | tf_op jit(solution)/shard_map/ppermute | solution.py:21
  90.6 0.8 fusion.154
  91.4 4.6 %collective-permute-done.9 = f32[4,5,16,256]{3,2,1,0:T(8,128)S(1)} collective-permute-done((f32[4,5,16,256]{3,2,1,0:T(8,128)S(1)}, f32[4,5,16,256]{3,2,1,0:T(8,128)S(1)}, u32[]{:S(2)}, u32[]{:S(2)}) %collective-permute-start.9) | collective-permute-done | bytes 327712 | tf_op jit(solution)/shard_map/ppermute | solution.py:22
  96.0 0.9 collective-permute-done.8
  97.0 1.1 fusion.127
  98.1 3.7 %collective-permute-start.11 = (f32[4,16,5,256]{3,2,1,0:T(8,128)}, f32[4,16,5,256]{3,2,1,0:T(8,128)}, u32[]{:S(2)}, u32[]{:S(2)}) collective-permute-start(f32[4,16,5,256]{3,2,1,0:T(8,128)} %get-tuple-element.136), channel_id=1, source_target_pairs={{1,0},{3,2},{5,4},{7,6},{9,8},{11,10},{13,12},{15,14},{17,16},{19,... | collective-permute-start | bytes 983048 | tf_op jit(solution)/shard_map/ppermute | solution.py:22
  101.8 1.3 collective-permute-start.10
  103.0 0.8 multiply_reduce_fusion.8
  103.9 24.3 %all-reduce.39 = (f32[]{:T(128)}, f32[1]{0:T(128)}) all-reduce(f32[]{:T(128)} %get-tuple-element.86, f32[1]{0:T(128)} %bitcast.25), channel_id=1, replica_groups=mesh['slab_0'=8,'slab_1'=4,'slab_2'=4,'sub'=2] {'slab_0'}, use_global_device_ids=true, to_apply=%region_11.12 | all-reduce | flops 2 | bytes 16 | tf_op jit(solution)/shard_map/psum | solution.py:28
  128.2 6.6 %all-reduce.45 = (f32[]{:T(128)}, f32[1]{0:T(128)}) all-reduce(f32[]{:T(128)} %get-tuple-element.91, f32[1]{0:T(128)} %get-tuple-element.92), channel_id=1, replica_groups=mesh['slab_0'=8,'slab_1'=4,'slab_2'=4,'sub'=2] {'slab_1'}, use_global_device_ids=true, to_apply=%region_12.13 | all-reduce | flops 2 | bytes 16 | tf_op jit(solution)/shard_map/psum | solution.py:28
  134.8 6.8 %all-reduce.42 = (f32[]{:T(128)}, f32[1]{0:T(128)}) all-reduce(f32[]{:T(128)} %get-tuple-element.103, f32[1]{0:T(128)} %get-tuple-element.104), channel_id=1, replica_groups=mesh['slab_0'=8,'slab_1'=4,'slab_2'=4,'sub'=2] {'slab_2'}, use_global_device_ids=true, to_apply=%region_13.14 | all-reduce | flops 2 | bytes 16 | tf_op jit(solution)/shard_map/psum | solution.py:28
  141.6 12.2 %all-reduce.48 = (f32[]{:T(128)}, f32[1]{0:T(128)}) all-reduce(f32[]{:T(128)} %get-tuple-element.97, f32[1]{0:T(128)} %get-tuple-element.98), channel_id=1, replica_groups=mesh['slab_0'=8,'slab_1'=4,'slab_2'=4,'sub'=2] {'sub'}, use_global_device_ids=true, to_apply=%region_14.15 | all-reduce | flops 2 | bytes 16 | tf_op jit(solution)/shard_map/psum | solution.py:28
  157.2 1.2 broadcast_multiply_fusion.1
  160.7 1.3 broadcast_divide_fusion.1
  165.9 2.2 multiply_reduce_fusion.6
  168.9 0.9 fusion.139
  169.8 1.3 collective-permute-start.13
  171.1 4.7 %collective-permute-start.12 = (f32[4,5,16,256]{3,2,1,0:T(8,128)}, f32[4,5,16,256]{3,2,1,0:T(8,128)}, u32[]{:S(2)}, u32[]{:S(2)}) collective-permute-start(f32[4,5,16,256]{3,2,1,0:T(8,128)} %get-tuple-element.162), channel_id=1, source_target_pairs={{0,2},{2,4},{4,6},{6,8},{8,10},{10,12},{12,14},{14,16},{16,18},{18... | collective-permute-start | bytes 983048 | tf_op jit(solution)/shard_map/ppermute | solution.py:21
  175.8 1.8 pad_maximum_fusion.29
  177.6 15.3 %all-reduce.38 = (f32[]{:T(128)}, f32[2]{0:T(128)}) all-reduce(f32[]{:T(128)} %get-tuple-element.83, f32[2]{0:T(128)} %pad_maximum_fusion.29), channel_id=1, replica_groups=mesh['slab_0'=8,'slab_1'=4,'slab_2'=4,'sub'=2] {'slab_0'}, use_global_device_ids=true, to_apply=%region_22.23 | all-reduce | flops 3 | bytes 24 | tf_op jit(solution)/shard_map/psum | solution.py:28
  192.9 7.1 %all-reduce.44 = (f32[]{:T(128)}, f32[2]{0:T(128)}) all-reduce(f32[]{:T(128)} %get-tuple-element.89, f32[2]{0:T(128)} %get-tuple-element.90), channel_id=1, replica_groups=mesh['slab_0'=8,'slab_1'=4,'slab_2'=4,'sub'=2] {'slab_1'}, use_global_device_ids=true, to_apply=%region_23.24 | all-reduce | flops 3 | bytes 24 | tf_op jit(solution)/shard_map/psum | solution.py:28
  200.0 12.2 %all-reduce.41 = (f32[]{:T(128)}, f32[2]{0:T(128)}) all-reduce(f32[]{:T(128)} %get-tuple-element.101, f32[2]{0:T(128)} %get-tuple-element.102), channel_id=1, replica_groups=mesh['slab_0'=8,'slab_1'=4,'slab_2'=4,'sub'=2] {'slab_2'}, use_global_device_ids=true, to_apply=%region_24.25 | all-reduce | flops 3 | bytes 24 | tf_op jit(solution)/shard_map/psum | solution.py:28
  212.2 10.8 %all-reduce.47 = (f32[]{:T(128)}, f32[2]{0:T(128)}) all-reduce(f32[]{:T(128)} %get-tuple-element.95, f32[2]{0:T(128)} %get-tuple-element.96), channel_id=1, replica_groups=mesh['slab_0'=8,'slab_1'=4,'slab_2'=4,'sub'=2] {'sub'}, use_global_device_ids=true, to_apply=%region_25.26 | all-reduce | flops 3 | bytes 24 | tf_op jit(solution)/shard_map/psum | solution.py:28
  223.0 1.2 multiply_reduce_fusion.11
  225.4 3.2 %broadcast_select_fusion.1 = f32[2,1]{0,1:T(1,128)} fusion(pred[]{:T(512)} %compare_reduce_fusion, f32[2]{0:T(128)} %get-tuple-element.108, f32[4,3]{0,1:T(4,128)} %copy-done.43, s32[]{:T(128)} %bitcast.68, s32[]{:T(128)} %bitcast.69), kind=kLoop, calls=%fused_computation.257 | loop fusion | flops 2 | bytes 33 | tf_op jit(solution)/shard_map/select.8
  228.7 2.7 scatter.24
  231.3 1.4 scatter.25
  232.7 1.3 pad_maximum_fusion.5
  234.1 2.3 collective-permute-start.15
  236.4 1.5 collective-permute-start.14
  239.2 1.0 collective-permute-done.14
  240.2 1.1 broadcast_multiply_fusion
  243.3 1.2 broadcast_divide_fusion
  248.5 3.0 multiply_reduce_fusion.3
  251.5 1.9 pad_maximum_fusion.30
  253.4 14.0 %all-reduce.37 = (f32[]{:T(128)}, f32[3]{0:T(128)S(1)}) all-reduce(f32[]{:T(128)} %get-tuple-element.79, f32[3]{0:T(128)S(1)} %pad_maximum_fusion.30), channel_id=1, replica_groups=mesh['slab_0'=8,'slab_1'=4,'slab_2'=4,'sub'=2] {'slab_0'}, use_global_device_ids=true, to_apply=%region_35.36 | all-reduce | flops 4 | bytes 32 | tf_op jit(solution)/shard_map/psum | solution.py:28
  267.4 6.6 %all-reduce.43 = (f32[]{:T(128)}, f32[3]{0:T(128)S(1)}) all-reduce(f32[]{:T(128)} %get-tuple-element.87, f32[3]{0:T(128)S(1)} %get-tuple-element.88), channel_id=1, replica_groups=mesh['slab_0'=8,'slab_1'=4,'slab_2'=4,'sub'=2] {'slab_1'}, use_global_device_ids=true, to_apply=%region_36.37 | all-reduce | flops 4 | bytes 32 | tf_op jit(solution)/shard_map/psum | solution.py:28
  274.0 6.6 %all-reduce.40 = (f32[]{:T(128)}, f32[3]{0:T(128)S(1)}) all-reduce(f32[]{:T(128)} %get-tuple-element.99, f32[3]{0:T(128)S(1)} %get-tuple-element.100), channel_id=1, replica_groups=mesh['slab_0'=8,'slab_1'=4,'slab_2'=4,'sub'=2] {'slab_2'}, use_global_device_ids=true, to_apply=%region_37.38 | all-reduce | flops 4 | bytes 32 | tf_op jit(solution)/shard_map/psum | solution.py:28
  280.7 10.1 %all-reduce.46 = (f32[]{:T(128)}, f32[3]{0:T(128)S(1)}) all-reduce(f32[]{:T(128)} %get-tuple-element.93, f32[3]{0:T(128)S(1)} %get-tuple-element.94), channel_id=1, replica_groups=mesh['slab_0'=8,'slab_1'=4,'slab_2'=4,'sub'=2] {'sub'}, use_global_device_ids=true, to_apply=%region_38.39 | all-reduce | flops 4 | bytes 32 | tf_op jit(solution)/shard_map/psum | solution.py:28
  293.4 2.0 broadcast_select_fusion
  295.4 1.4 scatter.26
  297.6 2.9 fusion.117
  300.6 1.2 pad_maximum_fusion.2
  301.8 2.1 divide_bitcast_fusion
  303.9 1.3 pad_maximum_fusion
  (185 shorter events, 24.7 us)
Async XLA Ops:
  0.6 56.2 %copy-start.41 = (f32[6,16,256]{2,1,0:T(8,128)S(1)}, f32[6,16,256]{2,1,0:T(8,128)}, u32[]{:S(2)}) copy-start(f32[6,16,256]{2,1,0:T(8,128)} %param.19) | copy-start | bytes 294916
  0.6 56.2 %copy-start.37 = (f32[6,16,256]{2,1,0:T(8,128)S(1)}, f32[6,16,256]{2,1,0:T(8,128)}, u32[]{:S(2)}) copy-start(f32[6,16,256]{2,1,0:T(8,128)} %param.18) | copy-start | bytes 294916
  0.7 56.2 %copy-start.7 = (f32[3,6,16,256]{3,2,1,0:T(8,128)S(1)}, f32[3,6,16,256]{3,2,1,0:T(8,128)}, u32[]{:S(2)}) copy-start(f32[3,6,16,256]{3,2,1,0:T(8,128)} %param.17) | copy-start | bytes 884740
  51.5 11.6 %copy-start.46 = (s32[2]{0:T(128)S(1)}, s32[2]{0:T(128)}, u32[]{:S(2)}) copy-start(s32[2]{0:T(128)} %constant.240.clone.1) | copy-start | bytes 28
  51.5 21.8 %collective-permute-start.1 = (f32[4,5,16,256]{3,2,1,0:T(8,128)S(1)}, f32[4,5,16,256]{3,2,1,0:T(8,128)S(1)}, u32[]{:S(2)}, u32[]{:S(2)}) collective-permute-start(f32[4,5,16,256]{3,2,1,0:T(8,128)S(1)} %get-tuple-element.167), channel_id=1, source_target_pairs={{2,0},{4,2},{6,4},{8,6},{10,8},{12,10},{14,12},{16,14},{18,16},{20... | collective-permute-start | bytes 983048 | tf_op jit(solution)/shard_map/ppermute | solution.py:22
  52.8 20.5 %collective-permute-start = (f32[4,5,16,256]{3,2,1,0:T(8,128)S(1)}, f32[4,5,16,256]{3,2,1,0:T(8,128)S(1)}, u32[]{:S(2)}, u32[]{:S(2)}) collective-permute-start(f32[4,5,16,256]{3,2,1,0:T(8,128)S(1)} %get-tuple-element.166), channel_id=1, source_target_pairs={{0,2},{2,4},{4,6},{6,8},{8,10},{10,12},{12,14},{14,16},{16,18},{18... | collective-permute-start | bytes 983048 | tf_op jit(solution)/shard_map/ppermute | solution.py:21
  57.0 10.7 %collective-permute-start.5 = (f32[5,3,16,256]{3,2,1,0:T(8,128)S(1)}, f32[5,3,16,256]{3,2,1,0:T(8,128)S(1)}, u32[]{:S(2)}, u32[]{:S(2)}) collective-permute-start(f32[5,3,16,256]{3,2,1,0:T(8,128)S(1)} %get-tuple-element.161), channel_id=1, source_target_pairs={{2,0},{4,2},{6,4},{8,6},{10,8},{12,10},{14,12},{16,14},{18,16},{20... | collective-permute-start | bytes 737288 | tf_op jit(solution)/shard_map/ppermute | solution.py:22
  58.3 10.3 %collective-permute-start.4 = (f32[5,3,16,256]{3,2,1,0:T(8,128)S(1)}, f32[5,3,16,256]{3,2,1,0:T(8,128)S(1)}, u32[]{:S(2)}, u32[]{:S(2)}) collective-permute-start(f32[5,3,16,256]{3,2,1,0:T(8,128)S(1)} %get-tuple-element.160), channel_id=1, source_target_pairs={{0,2},{2,4},{4,6},{6,8},{8,10},{10,12},{12,14},{14,16},{16,18},{18... | collective-permute-start | bytes 737288 | tf_op jit(solution)/shard_map/ppermute | solution.py:21
  62.3 21.2 %copy-start.28 = (f32[6,16,256]{2,1,0:T(8,128)}, f32[6,16,256]{2,1,0:T(8,128)S(1)}, u32[]{:S(2)}) copy-start(f32[6,16,256]{2,1,0:T(8,128)S(1)} %get-tuple-element.193) | copy-start | bytes 294916
  62.3 21.2 %copy-start.31 = (f32[6,16,256]{2,1,0:T(8,128)}, f32[6,16,256]{2,1,0:T(8,128)S(1)}, u32[]{:S(2)}) copy-start(f32[6,16,256]{2,1,0:T(8,128)S(1)} %get-tuple-element.194) | copy-start | bytes 294916
  62.4 21.2 %copy-start.34 = (f32[6,16,256]{2,1,0:T(8,128)}, f32[6,16,256]{2,1,0:T(8,128)S(1)}, u32[]{:S(2)}) copy-start(f32[6,16,256]{2,1,0:T(8,128)S(1)} %broadcast_add_fusion) | copy-start | bytes 294916
  68.5 9.4 %copy-start.40 = (f32[5,3,16,256]{3,2,1,0:T(8,128)}, f32[5,3,16,256]{3,2,1,0:T(8,128)S(1)}, u32[]{:S(2)}) copy-start(f32[5,3,16,256]{3,2,1,0:T(8,128)S(1)} %collective-permute-done.4) | copy-start | bytes 737284
  68.6 9.3 %collective-permute-start.7 = (f32[5,12,3,256]{3,2,1,0:T(4,128)S(1)}, f32[5,12,3,256]{3,2,1,0:T(4,128)S(1)}, u32[]{:S(2)}, u32[]{:S(2)}) collective-permute-start(f32[5,12,3,256]{3,2,1,0:T(4,128)S(1)} %get-tuple-element.140), channel_id=1, source_target_pairs={{1,0},{3,2},{5,4},{7,6},{9,8},{11,10},{13,12},{15,14},{17,16},{19,... | collective-permute-start | bytes 552968 | tf_op jit(solution)/shard_map/ppermute | solution.py:22
  72.0 5.9 %collective-permute-start.6 = (f32[5,12,3,256]{3,2,1,0:T(4,128)S(1)}, f32[5,12,3,256]{3,2,1,0:T(4,128)S(1)}, u32[]{:S(2)}, u32[]{:S(2)}) collective-permute-start(f32[5,12,3,256]{3,2,1,0:T(4,128)S(1)} %get-tuple-element.139), channel_id=1, source_target_pairs={{0,1},{2,3},{4,5},{6,7},{8,9},{10,11},{12,13},{14,15},{16,17},{18,... | collective-permute-start | bytes 552968 | tf_op jit(solution)/shard_map/ppermute | solution.py:21
  73.5 5.8 %collective-permute-start.3 = (f32[4,16,5,256]{3,2,1,0:T(8,128)S(1)}, f32[4,16,5,256]{3,2,1,0:T(8,128)S(1)}, u32[]{:S(2)}, u32[]{:S(2)}) collective-permute-start(f32[4,16,5,256]{3,2,1,0:T(8,128)S(1)} %get-tuple-element.138), channel_id=1, source_target_pairs={{1,0},{3,2},{5,4},{7,6},{9,8},{11,10},{13,12},{15,14},{17,16},{19,... | collective-permute-start | bytes 983048 | tf_op jit(solution)/shard_map/ppermute | solution.py:22
  76.6 3.8 %collective-permute-start.2 = (f32[4,16,5,256]{3,2,1,0:T(8,128)S(1)}, f32[4,16,5,256]{3,2,1,0:T(8,128)S(1)}, u32[]{:S(2)}, u32[]{:S(2)}) collective-permute-start(f32[4,16,5,256]{3,2,1,0:T(8,128)S(1)} %get-tuple-element.137), channel_id=1, source_target_pairs={{0,1},{2,3},{4,5},{6,7},{8,9},{10,11},{12,13},{14,15},{16,17},{18,... | collective-permute-start | bytes 983048 | tf_op jit(solution)/shard_map/ppermute | solution.py:21
  79.2 2.8 copy-start.8
  79.3 3.2 %copy-start.12 = (f32[8,18,256]{2,1,0:T(8,128)}, f32[8,18,256]{2,1,0:T(8,128)S(1)}, u32[]{:S(2)}) copy-start(f32[8,18,256]{2,1,0:T(8,128)S(1)} %get-tuple-element.129) | copy-start | bytes 442372
  79.3 3.2 %copy-start.15 = (f32[8,18,256]{2,1,0:T(8,128)}, f32[8,18,256]{2,1,0:T(8,128)S(1)}, u32[]{:S(2)}) copy-start(f32[8,18,256]{2,1,0:T(8,128)S(1)} %get-tuple-element.130) | copy-start | bytes 442372
  79.3 3.2 %copy-start.18 = (f32[8,18,256]{2,1,0:T(8,128)}, f32[8,18,256]{2,1,0:T(8,128)S(1)}, u32[]{:S(2)}) copy-start(f32[8,18,256]{2,1,0:T(8,128)S(1)} %get-tuple-element.131) | copy-start | bytes 442372
  79.3 3.2 %copy-start.21 = (f32[8,18,256]{2,1,0:T(8,128)}, f32[8,18,256]{2,1,0:T(8,128)S(1)}, u32[]{:S(2)}) copy-start(f32[8,18,256]{2,1,0:T(8,128)S(1)} %get-tuple-element.132) | copy-start | bytes 442372
  83.5 7.1 %copy-start = (f32[4,6,16,256]{3,2,1,0:T(8,128)S(1)}, f32[4,6,16,256]{3,2,1,0:T(8,128)}, u32[]{:S(2)}) copy-start(f32[4,6,16,256]{3,2,1,0:T(8,128)} %param.16) | copy-start | bytes 1179652
  83.8 76.1 %copy-start.1 = (f32[3,6,16,256]{3,2,1,0:T(8,128)}, f32[3,6,16,256]{3,2,1,0:T(8,128)S(1)}, u32[]{:S(2)}) copy-start(f32[3,6,16,256]{3,2,1,0:T(8,128)S(1)} %fusion.65) | copy-start | bytes 884740
  83.9 12.1 %collective-permute-start.9 = (f32[4,5,16,256]{3,2,1,0:T(8,128)S(1)}, f32[4,5,16,256]{3,2,1,0:T(8,128)S(1)}, u32[]{:S(2)}, u32[]{:S(2)}) collective-permute-start(f32[4,5,16,256]{3,2,1,0:T(8,128)S(1)} %get-tuple-element.165), channel_id=1, source_target_pairs={{2,0},{4,2},{6,4},{8,6},{10,8},{12,10},{14,12},{16,14},{18,16},{20... | collective-permute-start | bytes 983048 | tf_op jit(solution)/shard_map/ppermute | solution.py:22
  85.2 11.7 %collective-permute-start.8 = (f32[4,5,16,256]{3,2,1,0:T(8,128)S(1)}, f32[4,5,16,256]{3,2,1,0:T(8,128)S(1)}, u32[]{:S(2)}, u32[]{:S(2)}) collective-permute-start(f32[4,5,16,256]{3,2,1,0:T(8,128)S(1)} %get-tuple-element.164), channel_id=1, source_target_pairs={{0,2},{2,4},{4,6},{6,8},{8,10},{10,12},{12,14},{14,16},{16,18},{18... | collective-permute-start | bytes 983048 | tf_op jit(solution)/shard_map/ppermute | solution.py:21
  96.0 2.1 copy-start.24
  96.9 1.2 copy-start.26
  98.1 59.2 %collective-permute-start.11 = (f32[4,16,5,256]{3,2,1,0:T(8,128)}, f32[4,16,5,256]{3,2,1,0:T(8,128)}, u32[]{:S(2)}, u32[]{:S(2)}) collective-permute-start(f32[4,16,5,256]{3,2,1,0:T(8,128)} %get-tuple-element.136), channel_id=1, source_target_pairs={{1,0},{3,2},{5,4},{7,6},{9,8},{11,10},{13,12},{15,14},{17,16},{19,... | collective-permute-start | bytes 983048 | tf_op jit(solution)/shard_map/ppermute | solution.py:22
  101.8 55.5 %collective-permute-start.10 = (f32[4,16,5,256]{3,2,1,0:T(8,128)}, f32[4,16,5,256]{3,2,1,0:T(8,128)}, u32[]{:S(2)}, u32[]{:S(2)}) collective-permute-start(f32[4,16,5,256]{3,2,1,0:T(8,128)} %get-tuple-element.135), channel_id=1, source_target_pairs={{0,1},{2,3},{4,5},{6,7},{8,9},{10,11},{12,13},{14,15},{16,17},{18,... | collective-permute-start | bytes 983048 | tf_op jit(solution)/shard_map/ppermute | solution.py:21
  156.5 1.9 copy-start.43
  159.5 0.9 copy-start.9
  159.5 1.1 copy-start.25
  159.5 1.2 copy-start.27
  162.1 0.9 copy-start.13
  162.1 1.0 copy-start.16
  162.1 1.1 copy-start.19
  162.1 1.2 copy-start.22
  164.0 0.9 copy-start.29
  164.0 0.9 copy-start.32
  164.0 1.0 copy-start.35
  165.0 1.0 copy-start.2
  168.1 0.7 copy-start.4
  169.8 62.9 %collective-permute-start.13 = (f32[4,5,16,256]{3,2,1,0:T(8,128)}, f32[4,5,16,256]{3,2,1,0:T(8,128)}, u32[]{:S(2)}, u32[]{:S(2)}) collective-permute-start(f32[4,5,16,256]{3,2,1,0:T(8,128)} %get-tuple-element.163), channel_id=1, source_target_pairs={{2,0},{4,2},{6,4},{8,6},{10,8},{12,10},{14,12},{16,14},{18,16},{20... | collective-permute-start | bytes 983048 | tf_op jit(solution)/shard_map/ppermute | solution.py:22
  171.1 61.6 %collective-permute-start.12 = (f32[4,5,16,256]{3,2,1,0:T(8,128)}, f32[4,5,16,256]{3,2,1,0:T(8,128)}, u32[]{:S(2)}, u32[]{:S(2)}) collective-permute-start(f32[4,5,16,256]{3,2,1,0:T(8,128)} %get-tuple-element.162), channel_id=1, source_target_pairs={{0,2},{2,4},{4,6},{6,8},{8,10},{10,12},{12,14},{14,16},{16,18},{18... | collective-permute-start | bytes 983048 | tf_op jit(solution)/shard_map/ppermute | solution.py:21
  234.0 3.9 %copy-start.45 = (f32[2]{0:T(128)S(1)}, f32[2]{0:T(128)}, u32[]{:S(2)}) copy-start(f32[2]{0:T(128)} %get-tuple-element.108) | copy-start | bytes 28
  234.0 6.2 %copy-start.5 = (f32[4,6,16,256]{3,2,1,0:T(8,128)S(1)}, f32[4,6,16,256]{3,2,1,0:T(8,128)}, u32[]{:S(2)}) copy-start(f32[4,6,16,256]{3,2,1,0:T(8,128)} %copy-done.4) | copy-start | bytes 1179652
  234.1 5.1 %collective-permute-start.15 = (f32[4,16,5,256]{3,2,1,0:T(8,128)S(1)}, f32[4,16,5,256]{3,2,1,0:T(8,128)S(1)}, u32[]{:S(2)}, u32[]{:S(2)}) collective-permute-start(f32[4,16,5,256]{3,2,1,0:T(8,128)S(1)} %get-tuple-element.134), channel_id=1, source_target_pairs={{1,0},{3,2},{5,4},{7,6},{9,8},{11,10},{13,12},{15,14},{17,16},{19,... | collective-permute-start | bytes 983048 | tf_op jit(solution)/shard_map/ppermute | solution.py:22
  236.4 3.8 %collective-permute-start.14 = (f32[4,16,5,256]{3,2,1,0:T(8,128)S(1)}, f32[4,16,5,256]{3,2,1,0:T(8,128)S(1)}, u32[]{:S(2)}, u32[]{:S(2)}) collective-permute-start(f32[4,16,5,256]{3,2,1,0:T(8,128)S(1)} %get-tuple-element.133), channel_id=1, source_target_pairs={{0,1},{2,3},{4,5},{6,7},{8,9},{10,11},{12,13},{14,15},{16,17},{18,... | collective-permute-start | bytes 983048 | tf_op jit(solution)/shard_map/ppermute | solution.py:21
  242.3 0.9 copy-start.10
  244.5 0.9 copy-start.14
  244.5 1.0 copy-start.17
  244.5 1.1 copy-start.20
  244.5 1.2 copy-start.23
  246.4 0.9 copy-start.30
  246.4 0.9 copy-start.33
  246.4 1.0 copy-start.36
  247.4 1.0 copy-start.3
  247.4 1.1 copy-start.6
  248.5 44.9 %copy-start.44 = (f32[4,3]{0,1:T(4,128)S(1)}, f32[4,3]{0,1:T(4,128)}, u32[]{:S(2)}) copy-start(f32[4,3]{0,1:T(4,128)} %scatter.25) | copy-start | bytes 148
  248.5 49.1 %copy-start.42 = (f32[1,8,18,256]{3,2,1,0:T(8,128)S(1)}, f32[1,8,18,256]{3,2,1,0:T(8,128)}, u32[]{:S(2)}) copy-start(f32[1,8,18,256]{3,2,1,0:T(8,128)} %slice_bitcast_fusion.6) | copy-start | bytes 442372
  300.6 1.2 copy-start.11
  300.6 1.2 copy-start.39
  301.7 2.2 copy-start.38
where the time goes:
time: 307 us; the launch traced here: 305 us
  blocking collectives  180 us (59%)
  other arithmetic  43.7 us (14%)
  starting transfers between devices  40.4 us (13%)
  local copies, waits for them, and re-layouts  23.1 us (8%)
  waiting for transfers between devices  11.3 us (4%)
  between operations  6.88 us (2%)
    psum x16, blocking collectives, over_axes(): return functools.reduce(lax.psum, axes, shard)  180 us
    ppermute x8, starting transfers between devices, padded_2(): before = lax.ppermute(last, axis, up)  22.8 us
    ppermute x8, starting transfers between devices, padded_2(): after = lax.ppermute(leading, axis, down)  17.6 us
    another operation x5, other arithmetic, per_device(): return (jnp.stack(vectors), jnp.stack(searches), hess)  8.28 us
    unnamed x95, local copies, waits for them, and re-layouts  7.76 us
    ppermute x8, waiting for transfers between devices, padded_2(): after = lax.ppermute(leading, axis, down)  7.39 us
    another operation x5, other arithmetic  6.6 us
  transfers between devices with their start and end apart: 16, of which 6 were waited for; matrix products, arithmetic and copies ran while one was open for 6% of the time, Pallas kernels for 0%

commit v1 on v0

v1 whole, which is shorter than its diff:
```python
import functools

import jax
import jax.numpy as jnp
from jax import lax
from jax.experimental import pallas as pl
from jax.experimental.pallas import tpu as pltpu
from jax.sharding import PartitionSpec as P

MESH_ID = pl.DeviceIdType.MESH
NX_T, NY_T, NZ_T = 4, 4, 8
ROWS = 24
HALF = 128


def lane_is(lane):
    return lax.broadcasted_iota(jnp.int32, (ROWS, HALF), 1) == lane


def get(ref, *lead):
    return ref[(*lead, slice(None), pl.ds(0, HALF))], ref[(*lead, slice(None), pl.ds(HALF, HALF))]


def put(ref, value, *lead):
    ref[(*lead, slice(None), pl.ds(0, HALF))] = value[0]
    ref[(*lead, slice(None), pl.ds(HALF, HALF))] = value[1]


def up_z(f, last):
    low, high = pltpu.roll(f[0], HALF - 1, 1), pltpu.roll(f[1], HALF - 1, 1)
    return jnp.where(last, high, low), jnp.where(last, 0.0, high)


def down_z(f, first):
    low, high = pltpu.roll(f[0], 1, 1), pltpu.roll(f[1], 1, 1)
    return jnp.where(first, 0.0, low), jnp.where(first, low, high)


def up_y(f):
    return tuple(pltpu.roll(h, ROWS - 1, 0) for h in f)


def down_y(f):
    return tuple(pltpu.roll(h, 1, 0) for h in f)


def krylov_kernel(
    start, wind, reac, mass,
    w0_out, w1_out, w2_out, z0_out, z1_out, z2_out, gram_out,
    vec, coef, work, t1, q, res, y0, y1, w2, part, slots_a, slots_b, slots_c,
    send_sems, recv_sems, load_sems, store_sems,
):
    slab, sub = lax.axis_index("slab"), lax.axis_index("sub")
    slabs = lax.axis_size("slab")
    other = 1 - sub
    x, y, z = lax.rem(slab, NX_T), lax.rem(lax.div(slab, NX_T), NY_T), lax.div(slab, NX_T * NY_T)
    has_left, has_right = slab > 0, slab < slabs - 1
    left, right = jnp.maximum(slab - 1, 0), jnp.minimum(slab + 1, slabs - 1)
    own_rows = pl.ds(pl.multiple_of(8 * sub, 8), 16)
    out_tile = pl.ds(8, 8)
    in_tile = pl.ds(pl.multiple_of(16 * sub, 8), 8)
    hbm_tile = pl.ds(pl.multiple_of(8 * other, 8), 8)

    def peers(stage):
        if stage == 0:
            for k in range(1, 2 * NX_T):
                at = lax.rem(2 * x + sub + k, 2 * NX_T)
                yield (slab - x + lax.div(at, 2), lax.rem(at, 2))
        elif stage == 1:
            for k in range(1, NY_T):
                yield (slab + NX_T * (lax.rem(y + k, NY_T) - y), sub)
        else:
            for k in range(1, NZ_T):
                yield (slab + NX_T * NY_T * (lax.rem(z + k, NZ_T) - z), sub)

    loads = [
        pltpu.make_async_copy(start, vec.at[0, :, pl.ds(5, 6), own_rows], load_sems.at[0]),
        pltpu.make_async_copy(wind, coef.at[pl.ds(0, 3), pl.ds(3, 6), own_rows], load_sems.at[1]),
        pltpu.make_async_copy(reac, coef.at[3, pl.ds(3, 6), own_rows], load_sems.at[2]),
        pltpu.make_async_copy(mass, coef.at[4, pl.ds(3, 6), own_rows], load_sems.at[3]),
    ]
    for copy in loads:
        copy.start()

    barrier = pltpu.get_barrier_semaphore()
    count = 0
    for stage in range(3):
        for peer in peers(stage):
            pl.semaphore_signal(barrier, inc=1, device_id=peer, device_id_type=MESH_ID)
            count += 1

    @pl.when(has_left)
    def _():
        pl.semaphore_signal(barrier, inc=1, device_id=(left, sub), device_id_type=MESH_ID)

    @pl.when(has_right)
    def _():
        pl.semaphore_signal(barrier, inc=1, device_id=(right, sub), device_id_type=MESH_ID)

    def clear(planes, coef_planes):
        for k in range(3):
            for f in range(4):
                vec[k, f, planes] = jnp.zeros((5, ROWS, 256), jnp.float32)
        for f in range(5):
            coef[f, coef_planes] = jnp.zeros((3, ROWS, 256), jnp.float32)

    @pl.when(jnp.logical_not(has_left))
    def _():
        clear(pl.ds(0, 5), pl.ds(0, 3))

    @pl.when(jnp.logical_not(has_right))
    def _():
        clear(pl.ds(11, 5), pl.ds(9, 3))

    pl.semaphore_wait(
        barrier, count + has_left.astype(jnp.int32) + has_right.astype(jnp.int32)
    )

    used = [0]

    def remote(src, dst, device):
        at = used[0]
        used[0] += 1
        return pltpu.make_async_remote_copy(
            src_ref=src, dst_ref=dst, send_sem=send_sems.at[at], recv_sem=recv_sems.at[at],
            device_id=device, device_id_type=MESH_ID,
        )

    started = []

    def go(copy, condition=None):
        started.append((copy, condition))
        if condition is None:
            copy.start()
        else:
            pl.when(condition)(copy.start)

    def arrive(copy, condition=None):
        if condition is None:
            copy.wait_recv()
        else:
            pl.when(condition)(copy.wait_recv)

    class Halo:
        def __init__(self, src_low, src_high, src_tile, buffer, low, high, own):
            self.to_right = remote(src_high, buffer(low, own_rows), (right, sub))
            self.to_left = remote(src_low, buffer(high, own_rows), (left, sub))
            self.to_other = remote(src_tile, buffer(own, in_tile), (slab, other))
            self.low_on = remote(buffer(low, out_tile), buffer(low, in_tile), (slab, other))
            self.high_on = remote(buffer(high, out_tile), buffer(high, in_tile), (slab, other))

        def send(self):
            go(self.to_right, has_right)
            go(self.to_left, has_left)
            go(self.to_other)

        def forward(self):
            arrive(self.to_right, has_left)
            go(self.low_on, has_left)
            arrive(self.to_left, has_right)
            go(self.high_on, has_right)

        def finish(self):
            arrive(self.to_other)
            arrive(self.low_on, has_left)
            arrive(self.high_on, has_right)

    def vec_halo(k):
        def pressure(planes, rows):
            return vec.at[k, 3, planes, rows]

        def velocity(planes, rows):
            return vec.at[k, pl.ds(0, 3), planes, rows]

        if k == 0:
            p_src = (start.at[3, pl.ds(0, 5)], start.at[3, pl.ds(1, 5)], start.at[3, :, hbm_tile])
            u_src = tuple(
                start.at[pl.ds(0, 3), planes] for planes in (pl.ds(0, 2), pl.ds(4, 2))
            ) + (start.at[pl.ds(0, 3), :, hbm_tile],)
        else:
            p_src = (
                pressure(pl.ds(5, 5), own_rows), pressure(pl.ds(6, 5), own_rows),
                pressure(pl.ds(5, 6), out_tile),
            )
            u_src = (
                velocity(pl.ds(5, 2), own_rows), velocity(pl.ds(9, 2), own_rows),
                velocity(pl.ds(5, 6), out_tile),
            )
        p_halo = Halo(*p_src, pressure, pl.ds(0, 5), pl.ds(11, 5), pl.ds(5, 6))
        u_halo = Halo(*u_src, velocity, pl.ds(3, 2), pl.ds(11, 2), pl.ds(5, 6))
        return p_halo, u_halo

    def coef_halo(src, buffer):
        if len(src.shape) == 4:
            parts = (src.at[:, pl.ds(0, 3)], src.at[:, pl.ds(3, 3)], src.at[:, :, hbm_tile])
        else:
            parts = (src.at[pl.ds(0, 3)], src.at[pl.ds(3, 3)], src.at[:, hbm_tile])
        return Halo(*parts, buffer, pl.ds(0, 3), pl.ds(9, 3), pl.ds(3, 6))

    p_halo, u_halo = vec_halo(0)
    coef_halos = [
        coef_halo(wind, lambda planes, rows: coef.at[pl.ds(0, 3), planes, rows]),
        coef_halo(reac, lambda planes, rows: coef.at[3, planes, rows]),
        coef_halo(mass, lambda planes, rows: coef.at[4, planes, rows]),
    ]
    p_halo.send()
    for halo in coef_halos:
        halo.send()
    u_halo.send()

    last, first = lane_is(HALF - 1), lane_is(0)
    row = lax.broadcasted_iota(jnp.int32, (ROWS, HALF), 0)
    live = row != (ROWS - 1) * other

    def inside(plane):
        at = slab * 6 + plane - 5
        return jnp.logical_and(at >= 0, at < slabs * 6)

    def prepare(j, _):
        ok = jnp.logical_and(live, inside(j + 2))
        for d in range(3):
            half = [0.5 * h for h in get(coef, d, j)]
            put(work, [h - 1.0 for h in half], d, j)
            put(work, [-1.0 - h for h in half], d + 3, j)
        diagonal = [6.0 + h for h in get(coef, 3, j)]
        put(work, diagonal, 6, j)
        put(work, [jnp.where(ok, 1.0 / h, 0.0) for h in diagonal], 7, j)
        put(work, [jnp.where(ok, -1.0 / h, 0.0) for h in get(coef, 4, j)], 8, j)
        return 0

    def six(fxm, f, fxp):
        total = [a + b for a, b in zip(fxm, fxp)]
        for g in (up_y(f), down_y(f), up_z(f, last), down_z(f, first)):
            total = [a + b for a, b in zip(total, g)]
        return total

    def weights(j):
        return [get(work, i, j) for i in range(7)]

    def transport(fxm, f, fxp, w):
        total = [a * b for a, b in zip(w[6], f)]
        terms = ((0, fxp), (3, fxm), (1, up_y(f)), (4, down_y(f)), (2, up_z(f, last)), (5, down_z(f, first)))
        for i, g in terms:
            total = [t + a * b for t, a, b in zip(total, w[i], g)]
        return total

    def half_difference(a, b):
        return [0.5 * (m - n) for m, n in zip(a, b)]

    def gradient(fxm, f, fxp):
        return (
            half_difference(fxp, fxm),
            half_difference(up_y(f), down_y(f)),
            half_difference(up_z(f, last), down_z(f, first)),
        )

    def pressure_part(k):
        def masked(j):
            return [jnp.where(live, h, 0.0) for h in get(vec, k, 3, j)]

        def guess(j, _):
            scale = jnp.where(jnp.logical_and(live, inside(j)), 1.0 / 49.0, 0.0)
            f = masked(j)
            total = six(get(vec, k, 3, j - 1), f, get(vec, k, 3, j + 1))
            put(t1, [scale * (7.0 * a + b) for a, b in zip(f, total)], j)
            return 0

        lax.fori_loop(1, 15, guess, 0)

        def schur(j, _):
            value = transport(get(t1, j + 1), get(t1, j + 2), get(t1, j + 3), weights(j))
            put(q, [a * b for a, b in zip(value, get(work, 8, j))], k, j)
            return 0

        lax.fori_loop(0, 12, schur, 0)

    def velocity_part(k, target):
        def first_guess(j, _):
            slope = gradient(get(q, k, j), get(q, k, j + 1), get(q, k, j + 2))
            inverse = get(work, 7, j + 1)
            for d in range(3):
                r = [a - b for a, b in zip(get(vec, k, d, j + 3), slope[d])]
                put(res, r, d, j)
                put(y0, [a * b for a, b in zip(r, inverse)], d, j)
            return 0

        lax.fori_loop(0, 10, first_guess, 0)

        def second_guess(j, _):
            w = weights(j + 2)
            inverse = get(work, 7, j + 2)
            for d in range(3):
                f = get(y0, d, j + 1)
                value = transport(get(y0, d, j), f, get(y0, d, j + 2), w)
                r = get(res, d, j + 1)
                put(y1, [a + (b - c) * i for a, b, c, i in zip(f, r, value, inverse)], k, d, j)
            return 0

        lax.fori_loop(0, 8, second_guess, 0)

        def store(f, j, value):
            for i, h in enumerate(value):
                mine = jnp.where(sub == 0, h[0:16], h[8:24])
                target(f, j)[own_rows if k < 2 else slice(None), pl.ds(HALF * i, HALF)] = mine

        def image(j, _):
            w = weights(j + 3)
            pm, pc, pp = get(q, k, j + 2), get(q, k, j + 3), get(q, k, j + 4)
            slope = gradient(pm, pc, pp)
            flow = None
            for d in range(3):
                fm, f, fp = get(y1, k, d, j), get(y1, k, d, j + 1), get(y1, k, d, j + 2)
                value = transport(fm, f, fp, w)
                store(d, j, [a + b for a, b in zip(value, slope[d])])
                ends = ((fp, fm), (up_y(f), down_y(f)), (up_z(f, last), down_z(f, first)))[d]
                part_flow = [a - b for a, b in zip(*ends)]
                flow = part_flow if flow is None else [a + b for a, b in zip(flow, part_flow)]
            total = six(pm, pc, pp)
            store(3, j, [-0.5 * (a + (6.0 * b - c)) for a, b, c in zip(flow, pc, total)])
            return 0

        lax.fori_loop(0, 6, image, 0)

    lane8 = lax.broadcasted_iota(jnp.int32, (8, HALF), 1)

    def vectors(i, f, j):
        if i < 3:
            block = vec[i, f, 5 + j, own_rows, :]
        else:
            block = w2[f, j]
        return block

    def dots(new, olds):
        def step(i, accs):
            f, j = lax.div(i, 6), lax.rem(i, 6)
            b = vectors(new, f, j)
            out = []
            for acc, old in zip(accs, olds):
                prod = b * (b if old == new else vectors(old, f, j))
                out.append(acc + ((prod[0:8, 0:HALF] + prod[0:8, HALF:]) + (prod[8:16, 0:HALF] + prod[8:16, HALF:])))
            return tuple(out)

        zero = jnp.zeros((8, HALF), jnp.float32)
        return lax.fori_loop(0, 24, step, tuple(zero for _ in olds))

    def pack(total, sums, at):
        for i, s in enumerate(sums):
            total = jnp.where(lane8 == at + i, jnp.sum(s, axis=1, keepdims=True), total)
        return total

    for copy in loads:
        copy.wait()
    p_halo.forward()
    for halo in coef_halos:
        halo.forward()
    p_halo.finish()
    for halo in coef_halos:
        halo.finish()
    lax.fori_loop(0, 12, prepare, 0)
    pressure_part(0)
    u_halo.forward()
    u_halo.finish()
    velocity_part(0, lambda f, j: vec.at[1, f, 5 + j])

    stores = []

    def save(src, dst):
        copy = pltpu.make_async_copy(src, dst, store_sems.at[len(stores)])
        copy.start()
        stores.append(copy)

    gram = jnp.zeros((8, HALF), jnp.float32)
    at = 0
    for k, (w_out, z_out) in enumerate(((w0_out, z0_out), (w1_out, z1_out))):
        p_halo, u_halo = vec_halo(k + 1)
        p_halo.send()
        u_halo.send()
        save(vec.at[k + 1, :, pl.ds(5, 6), own_rows], w_out)
        save(y1.at[k, :, pl.ds(1, 6), own_rows], z_out.at[pl.ds(0, 3)])
        save(q.at[k, pl.ds(3, 6), own_rows], z_out.at[3])
        if k == 0:
            gram = pack(gram, dots(0, (0,)), 0)
            at = 1
        olds = tuple(range(k + 2))
        gram = pack(gram, dots(k + 1, olds), at)
        at += len(olds)
        p_halo.forward()
        p_halo.finish()
        pressure_part(k + 1)
        u_halo.forward()
        u_halo.finish()
        velocity_part(k + 1, (lambda f, j: vec.at[2, f, 5 + j]) if k == 0 else (lambda f, j: w2.at[f, j]))
    gram = pack(gram, dots(3, (0, 1, 2, 3)), at)
    save(y1.at[2, :, pl.ds(1, 6), own_rows], z2_out.at[pl.ds(0, 3)])
    save(q.at[2, pl.ds(3, 6), own_rows], z2_out.at[3])
    save(w2, w2_out)

    places = (2 * x + sub, y, z)
    for stage, slots in enumerate((slots_a, slots_b, slots_c)):
        place = places[stage]
        part[stage] = gram
        slots[place] = gram
        copies = [remote(part.at[stage], slots.at[place], peer) for peer in peers(stage)]
        for copy in copies:
            go(copy)
        for copy in copies:
            arrive(copy)
        gram = slots[0]
        for i in range(1, slots.shape[0]):
            gram = gram + slots[i]
    gram_out[...] = gram

    for copy, condition in started:
        if condition is None:
            copy.wait_send()
        else:
            pl.when(condition)(copy.wait_send)
    for copy in stores:
        copy.wait()


def combine_kernel(
    start, w0, w1, w2, z0, z1, z2, gram, basis, search, hess, y_in, z_in, b_out, s_out, in_sems, out_sems
):
    reads = []
    for f in range(4):
        group = []
        for i, src in enumerate((start, w0, w1, w2)):
            group.append(pltpu.make_async_copy(src.at[f], y_in.at[i, f], in_sems.at[f, i]))
        for i, src in enumerate((z0, z1, z2)):
            group.append(pltpu.make_async_copy(src.at[f], z_in.at[i, f], in_sems.at[f, 4 + i]))
        for copy in group:
            copy.start()
        reads.append(group)

    total = jnp.sum(gram[...], axis=0, keepdims=True)
    lane = lax.broadcasted_iota(jnp.int32, (1, HALF), 1)

    def entry(i):
        return jnp.broadcast_to(jnp.sum(jnp.where(lane == i, total, 0.0), axis=1, keepdims=True), (1, HALF))

    low = {}
    inverse = {}
    for i in range(4):
        for j in range(i + 1):
            value = entry(i * (i + 1) // 2 + j)
            for m in range(j):
                value = value - low[i, m] * low[j, m]
            if i == j:
                low[i, i] = jnp.sqrt(value)
                inverse[i] = 1.0 / low[i, i]
            else:
                low[i, j] = value * inverse[j]
    h = {}
    for j in range(3):
        for i in range(j + 2):
            value = low[j + 1, i]
            for m in range(j):
                if i <= m + 1:
                    value = value - low[j, m] * h[i, m]
            h[i, j] = value * inverse[j]
    at_row = lax.broadcasted_iota(jnp.int32, (4, HALF), 0)
    at_col = lax.broadcasted_iota(jnp.int32, (4, HALF), 1)
    table = jnp.zeros((4, HALF), jnp.float32)
    for (i, j), value in h.items():
        table = jnp.where(jnp.logical_and(at_row == i, at_col == j), value, table)
    hess[...] = table[:, 0:3]

    def wide(v):
        return jnp.concatenate([v, v], axis=1)

    scale = {key: wide(v) for key, v in low.items()}
    inv = {key: wide(v) for key, v in inverse.items()}

    writes = []
    for f in range(4):
        for copy in reads[f]:
            copy.wait()

        def body(j, _):
            for src, dst, n in ((y_in, b_out, 4), (z_in, s_out, 3)):
                done = []
                for i in range(n):
                    value = src[i, f, j]
                    for m in range(i):
                        value = value - scale[i, m] * done[m]
                    value = value * inv[i]
                    dst[i, f, j] = value
                    done.append(value)
            return 0

        lax.fori_loop(0, 6, body, 0)
        for i, (src, dst) in enumerate(((b_out, basis), (s_out, search))):
            copy = pltpu.make_async_copy(src.at[:, f], dst.at[:, f], out_sems.at[f, i])
            copy.start()
            writes.append(copy)
    for copy in writes:
        copy.wait()


def per_device(start, wind, reaction, mass):
    f32 = jnp.float32
    block = jax.ShapeDtypeStruct((4, 6, 16, 256), f32)
    any_spec = pl.BlockSpec(memory_space=pl.ANY)
    vmem_spec = pl.BlockSpec(memory_space=pltpu.VMEM)
    n_remote = 10 * 3 + 15 + 7 + 3 + 7
    outs = pl.pallas_call(
        krylov_kernel,
        out_shape=(block,) * 6 + (jax.ShapeDtypeStruct((8, HALF), f32),),
        in_specs=[any_spec] * 4,
        out_specs=(any_spec,) * 6 + (vmem_spec,),
        scratch_shapes=[
            pltpu.VMEM((3, 4, 16, ROWS, 256), f32),
            pltpu.VMEM((5, 12, ROWS, 256), f32),
            pltpu.VMEM((9, 12, ROWS, 256), f32),
            pltpu.VMEM((16, ROWS, 256), f32),
            pltpu.VMEM((3, 12, ROWS, 256), f32),
            pltpu.VMEM((3, 10, ROWS, 256), f32),
            pltpu.VMEM((3, 10, ROWS, 256), f32),
            pltpu.VMEM((3, 3, 8, ROWS, 256), f32),
            pltpu.VMEM((4, 6, 16, 256), f32),
            pltpu.VMEM((3, 8, HALF), f32),
            pltpu.VMEM((8, 8, HALF), f32),
            pltpu.VMEM((4, 8, HALF), f32),
            pltpu.VMEM((8, 8, HALF), f32),
            pltpu.SemaphoreType.DMA((n_remote,)),
            pltpu.SemaphoreType.DMA((n_remote,)),
            pltpu.SemaphoreType.DMA((4,)),
            pltpu.SemaphoreType.DMA((9,)),
        ],
        compiler_params=pltpu.CompilerParams(
            collective_id=0, has_side_effects=True, vmem_limit_bytes=40 * 2**20
        ),
        name="krylov",
    )(start, wind, reaction, mass)
    return tuple(pl.pallas_call(
        combine_kernel,
        out_shape=(
            jax.ShapeDtypeStruct((4, 4, 6, 16, 256), f32),
            jax.ShapeDtypeStruct((3, 4, 6, 16, 256), f32),
            jax.ShapeDtypeStruct((4, 3), f32),
        ),
        in_specs=[any_spec] * 7 + [vmem_spec],
        out_specs=(any_spec, any_spec, vmem_spec),
        scratch_shapes=[
            pltpu.VMEM((4, 4, 6, 16, 256), f32),
            pltpu.VMEM((3, 4, 6, 16, 256), f32),
            pltpu.VMEM((4, 4, 6, 16, 256), f32),
            pltpu.VMEM((3, 4, 6, 16, 256), f32),
            pltpu.SemaphoreType.DMA((4, 7)),
            pltpu.SemaphoreType.DMA((4, 2)),
        ],
        name="combine",
    )(start, *outs))


def solution(mesh):
    in_specs = (
        P(None, "slab", "sub", None),
        P(None, "slab", "sub", None),
        P("slab", "sub", None),
        P("slab", "sub", None),
    )
    out_specs = (P(None, None, "slab", "sub", None), P(None, None, "slab", "sub", None), P())
    return jax.shard_map(per_device, mesh=mesh, in_specs=in_specs, out_specs=out_specs, check_vma=False)
```

time: 307 us -> 81.5 us (0.27)
  blocking collectives: 180 us -> 0 us
  Pallas kernels: 0 us -> 71.7 us
  other arithmetic: 43.7 us -> 0 us
  starting transfers between devices: 40.4 us -> 0 us
  local copies, waits for them, and re-layouts: 23.1 us -> 8.81 us
  waiting for transfers between devices: 11.3 us -> 0 us
  between operations: 6.88 us -> 0.67 us
    psum x16 -> x0, blocking collectives: 180 us -> none  [over_axes(): return functools.reduce(lax.psum, axes, shard)]
    pallas_call x0 -> x2, Pallas kernels: none -> 71.7 us  [the longest x1 67.3 us: per_device(): pl.pallas_call(krylov_kernel, out_shape=(block,) * 6 + (jax.ShapeDtypeStr...]
    ppermute x16 -> x0, starting transfers between devices: 40.4 us -> none  [the longest x8 22.8 us: padded_2(): before = lax.ppermute(last, axis, up)]
    another operation x20 -> x0, other arithmetic: 19.6 us -> none  [the longest x5 8.28 us: per_device(): return (jnp.stack(vectors), jnp.stack(searches), hess)]
    ppermute x16 -> x0, waiting for transfers between devices: 11.3 us -> none  [the longest x8 7.39 us: padded_2(): after = lax.ppermute(leading, axis, down)]
    reduce_sum x6 -> x0, other arithmetic: 9.6 us -> none  [the longest x3 5.99 us: local_dots(): return jnp.stack([jnp.sum(vector * image) for vector in vectors])]
    slice x26 -> x0, local copies, waits for them, and re-layouts: 6.3 us -> none  [the longest x6 2.32 us: padded_2(): last = lax.slice_in_dim(shard, length - width, length, axis=dim)]
    scatter x6 -> x0, local copies, waits for them, and re-layouts: 6.29 us -> none  [the longest x3 4.71 us: per_device(): hess = hess.at[:column + 1, column].set(projected)]
  transfers between devices with their start and end apart: 16 -> 0, of which waited for: 6 -> 0; matrix products, arithmetic and copies ran while one was open for 6% -> 0% of each run, Pallas kernels for 0% -> 0%
where the time goes in v1:
time: 81.5 us; the launch traced here: 81.1 us
  Pallas kernels  71.7 us (88%)
  local copies, waits for them, and re-layouts  8.81 us (11%)
    pallas_call x1, Pallas kernels, per_device(): pl.pallas_call(krylov_kernel, out_shape=(block,) * 6 + (jax.ShapeDtypeStr...  67.3 us
    unnamed x22, local copies, waits for them, and re-layouts  8.81 us
    pallas_call x1, Pallas kernels, per_device(): pl.pallas_call(combine_kernel, out_shape=(jax.ShapeDtypeStruct((4, 4, 6,...  4.38 us

profile of v1, /device:TPU:1, one launch (start us, length us, event | category | flops | bytes accessed | tf_op | source)
XLA Modules:
  0.0 81.1 jit_solution(17257148675148597088)
XLA Ops:
  0.6 0.0 copy-start
  0.6 1.0 %copy-done = f32[4,6,16,256]{3,2,1,0:T(8,128)S(1)} copy-done((f32[4,6,16,256]{3,2,1,0:T(8,128)S(1)}, f32[4,6,16,256]{3,2,1,0:T(8,128)}, u32[]{:S(2)}) %copy-start) | copy-done | bytes 393240
  1.6 0.0 copy-start.7
  1.6 1.0 %copy-done.7 = f32[3,6,16,256]{3,2,1,0:T(8,128)S(1)} copy-done((f32[3,6,16,256]{3,2,1,0:T(8,128)S(1)}, f32[3,6,16,256]{3,2,1,0:T(8,128)}, u32[]{:S(2)}) %copy-start.7) | copy-done | bytes 294936
  2.6 0.0 copy-start.8
  2.6 0.9 %copy-done.8 = f32[6,16,256]{2,1,0:T(8,128)S(1)} copy-done((f32[6,16,256]{2,1,0:T(8,128)S(1)}, f32[6,16,256]{2,1,0:T(8,128)}, u32[]{:S(2)}) %copy-start.8) | copy-done | bytes 98328
  3.5 0.0 copy-start.9
  3.5 0.9 %copy-done.9 = f32[6,16,256]{2,1,0:T(8,128)S(1)} copy-done((f32[6,16,256]{2,1,0:T(8,128)S(1)}, f32[6,16,256]{2,1,0:T(8,128)}, u32[]{:S(2)}) %copy-start.9) | copy-done | bytes 98328
  4.4 67.3 %krylov.1 = (f32[4,6,16,256]{3,2,1,0:T(8,128)S(1)}, f32[4,6,16,256]{3,2,1,0:T(8,128)S(1)}, f32[4,6,16,256]{3,2,1,0:T(8,128)S(1)}, f32[4,6,16,256]{3,2,1,0:T(8,12...) custom-call(f32[4,6,16,256]{3,2,1,0:T(8,128)S(1)} %copy-done, ...), custom_call_target="tpu_custom_call" | custom-call | tf_op jit(solution)/shard_map/krylov/pallas_call | solution.py:507
  71.7 0.0 copy-start.1
  71.7 0.7 copy-done.1
  72.4 0.0 copy-start.2
  72.4 0.7 copy-done.2
  73.2 0.0 copy-start.3
  73.2 0.8 copy-done.3
  73.9 0.0 copy-start.4
  73.9 0.8 copy-done.4
  74.7 0.0 copy-start.5
  74.7 0.7 copy-done.5
  75.4 0.0 copy-start.6
  75.4 0.7 copy-done.6
  76.2 0.0 copy-start.10
  76.2 0.6 copy-done.10
  76.8 4.4 %combine.1 = (f32[4,4,6,16,256]{4,3,2,1,0:T(8,128)}, f32[3,4,6,16,256]{4,3,2,1,0:T(8,128)}, f32[4,3]{1,0:T(4,128)}) custom-call(f32[4,6,16,256]{3,2,1,0:T(8,128)} %start.3, f32[4,6,16,256]{3,2,1,0:T(8,128)} %copy-done.1, f32[4,6,16,256]{3,2,1,0:T(8,128)} %copy-done.2, f32[4,6,16,256]{3,2,1,0:T(8,128)} %copy-done.3, f32[4,6,16,256]{3,2,1,0:T(8,128)} %copy-done.4, ...), custom_call_target="tpu_custom_call" | custom-call | tf_op jit(solution)/shard_map/combine/pallas_call | solution.py:536
Async XLA Ops:
  0.6 1.0 %copy-start = (f32[4,6,16,256]{3,2,1,0:T(8,128)S(1)}, f32[4,6,16,256]{3,2,1,0:T(8,128)}, u32[]{:S(2)}) copy-start(f32[4,6,16,256]{3,2,1,0:T(8,128)} %start.3) | copy-start | bytes 1179652
  1.6 1.0 %copy-start.7 = (f32[3,6,16,256]{3,2,1,0:T(8,128)S(1)}, f32[3,6,16,256]{3,2,1,0:T(8,128)}, u32[]{:S(2)}) copy-start(f32[3,6,16,256]{3,2,1,0:T(8,128)} %wind.1) | copy-start | bytes 884740
  2.6 0.9 %copy-start.8 = (f32[6,16,256]{2,1,0:T(8,128)S(1)}, f32[6,16,256]{2,1,0:T(8,128)}, u32[]{:S(2)}) copy-start(f32[6,16,256]{2,1,0:T(8,128)} %reac.1) | copy-start | bytes 294916
  3.5 0.9 %copy-start.9 = (f32[6,16,256]{2,1,0:T(8,128)S(1)}, f32[6,16,256]{2,1,0:T(8,128)}, u32[]{:S(2)}) copy-start(f32[6,16,256]{2,1,0:T(8,128)} %mass.1) | copy-start | bytes 294916
  71.7 0.7 copy-start.1
  72.4 0.7 copy-start.2
  73.2 0.8 copy-start.3
  73.9 0.8 copy-start.4
  74.7 0.7 copy-start.5
  75.4 0.7 copy-start.6
  76.2 0.6 copy-start.10

commit v2 on v1

--- a/solution.py
+++ b/solution.py
@@ -46,9 +46,9 @@
 
 def krylov_kernel(
     start, wind, reac, mass,
-    w0_out, w1_out, w2_out, z0_out, z1_out, z2_out, gram_out,
-    vec, coef, work, t1, q, res, y0, y1, w2, part, slots_a, slots_b, slots_c,
-    send_sems, recv_sems, load_sems, store_sems,
+    vec, w2, y1, q, gram_out,
+    coef, work, t1, res, y0, part, slots_a, slots_b, slots_c,
+    send_sems, recv_sems, load_sems,
 ):
     slab, sub = lax.axis_index("slab"), lax.axis_index("sub")
     slabs = lax.axis_size("slab")
@@ -362,22 +362,12 @@
     u_halo.finish()
     velocity_part(0, lambda f, j: vec.at[1, f, 5 + j])
 
-    stores = []
-
-    def save(src, dst):
-        copy = pltpu.make_async_copy(src, dst, store_sems.at[len(stores)])
-        copy.start()
-        stores.append(copy)
-
     gram = jnp.zeros((8, HALF), jnp.float32)
     at = 0
-    for k, (w_out, z_out) in enumerate(((w0_out, z0_out), (w1_out, z1_out))):
+    for k in range(2):
         p_halo, u_halo = vec_halo(k + 1)
         p_halo.send()
         u_halo.send()
-        save(vec.at[k + 1, :, pl.ds(5, 6), own_rows], w_out)
-        save(y1.at[k, :, pl.ds(1, 6), own_rows], z_out.at[pl.ds(0, 3)])
-        save(q.at[k, pl.ds(3, 6), own_rows], z_out.at[3])
         if k == 0:
             gram = pack(gram, dots(0, (0,)), 0)
             at = 1
@@ -391,9 +381,6 @@
         u_halo.finish()
         velocity_part(k + 1, (lambda f, j: vec.at[2, f, 5 + j]) if k == 0 else (lambda f, j: w2.at[f, j]))
     gram = pack(gram, dots(3, (0, 1, 2, 3)), at)
-    save(y1.at[2, :, pl.ds(1, 6), own_rows], z2_out.at[pl.ds(0, 3)])
-    save(q.at[2, pl.ds(3, 6), own_rows], z2_out.at[3])
-    save(w2, w2_out)
 
     places = (2 * x + sub, y, z)
     for stage, slots in enumerate((slots_a, slots_b, slots_c)):
@@ -415,23 +402,10 @@
             copy.wait_send()
         else:
             pl.when(condition)(copy.wait_send)
-    for copy in stores:
-        copy.wait()
-
-
-def combine_kernel(
-    start, w0, w1, w2, z0, z1, z2, gram, basis, search, hess, y_in, z_in, b_out, s_out, in_sems, out_sems
-):
-    reads = []
-    for f in range(4):
-        group = []
-        for i, src in enumerate((start, w0, w1, w2)):
-            group.append(pltpu.make_async_copy(src.at[f], y_in.at[i, f], in_sems.at[f, i]))
-        for i, src in enumerate((z0, z1, z2)):
-            group.append(pltpu.make_async_copy(src.at[f], z_in.at[i, f], in_sems.at[f, 4 + i]))
-        for copy in group:
-            copy.start()
-        reads.append(group)
+
+
+def combine_kernel(vec, w2, y1, q, gram, basis, search, hess, b_out, s_out, out_sems):
+    own_rows = pl.ds(pl.multiple_of(8 * lax.axis_index("sub"), 8), 16)
 
     total = jnp.sum(gram[...], axis=0, keepdims=True)
     lane = lax.broadcasted_iota(jnp.int32, (1, HALF), 1)
@@ -474,14 +448,13 @@
 
     writes = []
     for f in range(4):
-        for copy in reads[f]:
-            copy.wait()
 
         def body(j, _):
-            for src, dst, n in ((y_in, b_out, 4), (z_in, s_out, 3)):
+            raw = [vec[i, f, 5 + j, own_rows, :] for i in range(3)] + [w2[f, j]]
+            found = [y1[i, f, 1 + j, own_rows, :] if f < 3 else q[i, 3 + j, own_rows, :] for i in range(3)]
+            for values, dst in ((raw, b_out), (found, s_out)):
                 done = []
-                for i in range(n):
-                    value = src[i, f, j]
+                for i, value in enumerate(values):
                     for m in range(i):
                         value = value - scale[i, m] * done[m]
                     value = value * inv[i]
@@ -500,25 +473,28 @@
 
 def per_device(start, wind, reaction, mass):
     f32 = jnp.float32
-    block = jax.ShapeDtypeStruct((4, 6, 16, 256), f32)
-    any_spec = pl.BlockSpec(memory_space=pl.ANY)
+    hbm_spec = pl.BlockSpec(memory_space=pltpu.HBM)
     vmem_spec = pl.BlockSpec(memory_space=pltpu.VMEM)
     n_remote = 10 * 3 + 15 + 7 + 3 + 7
+    kept = (
+        jax.ShapeDtypeStruct((3, 4, 16, ROWS, 256), f32),
+        jax.ShapeDtypeStruct((4, 6, 16, 256), f32),
+        jax.ShapeDtypeStruct((3, 3, 8, ROWS, 256), f32),
+        jax.ShapeDtypeStruct((3, 12, ROWS, 256), f32),
+        jax.ShapeDtypeStruct((8, HALF), f32),
+    )
+    arrays = [pltpu.with_memory_space_constraint(a, pltpu.HBM) for a in (start, wind, reaction, mass)]
     outs = pl.pallas_call(
         krylov_kernel,
-        out_shape=(block,) * 6 + (jax.ShapeDtypeStruct((8, HALF), f32),),
-        in_specs=[any_spec] * 4,
-        out_specs=(any_spec,) * 6 + (vmem_spec,),
+        out_shape=kept,
+        in_specs=[hbm_spec] * 4,
+        out_specs=(vmem_spec,) * 5,
         scratch_shapes=[
-            pltpu.VMEM((3, 4, 16, ROWS, 256), f32),
             pltpu.VMEM((5, 12, ROWS, 256), f32),
             pltpu.VMEM((9, 12, ROWS, 256), f32),
             pltpu.VMEM((16, ROWS, 256), f32),
-            pltpu.VMEM((3, 12, ROWS, 256), f32),
             pltpu.VMEM((3, 10, ROWS, 256), f32),
             pltpu.VMEM((3, 10, ROWS, 256), f32),
-            pltpu.VMEM((3, 3, 8, ROWS, 256), f32),
-            pltpu.VMEM((4, 6, 16, 256), f32),
             pltpu.VMEM((3, 8, HALF), f32),
             pltpu.VMEM((8, 8, HALF), f32),
             pltpu.VMEM((4, 8, HALF), f32),
@@ -526,13 +502,12 @@
             pltpu.SemaphoreType.DMA((n_remote,)),
             pltpu.SemaphoreType.DMA((n_remote,)),
             pltpu.SemaphoreType.DMA((4,)),
-            pltpu.SemaphoreType.DMA((9,)),
         ],
         compiler_params=pltpu.CompilerParams(
-            collective_id=0, has_side_effects=True, vmem_limit_bytes=40 * 2**20
+            collective_id=0, has_side_effects=True, vmem_limit_bytes=24 * 2**20
         ),
         name="krylov",
-    )(start, wind, reaction, mass)
+    )(*arrays)
     return tuple(pl.pallas_call(
         combine_kernel,
         out_shape=(
@@ -540,18 +515,16 @@
             jax.ShapeDtypeStruct((3, 4, 6, 16, 256), f32),
             jax.ShapeDtypeStruct((4, 3), f32),
         ),
-        in_specs=[any_spec] * 7 + [vmem_spec],
-        out_specs=(any_spec, any_spec, vmem_spec),
+        in_specs=[vmem_spec] * 5,
+        out_specs=(hbm_spec, hbm_spec, vmem_spec),
         scratch_shapes=[
             pltpu.VMEM((4, 4, 6, 16, 256), f32),
             pltpu.VMEM((3, 4, 6, 16, 256), f32),
-            pltpu.VMEM((4, 4, 6, 16, 256), f32),
-            pltpu.VMEM((3, 4, 6, 16, 256), f32),
-            pltpu.SemaphoreType.DMA((4, 7)),
             pltpu.SemaphoreType.DMA((4, 2)),
         ],
+        compiler_params=pltpu.CompilerParams(vmem_limit_bytes=24 * 2**20),
         name="combine",
-    )(start, *outs))
+    )(*outs))
 
 
 def solution(mesh):

time: 81.5 us -> 70.3 us (0.86)
  local copies, waits for them, and re-layouts: 8.81 us -> 0 us
  Pallas kernels: 71.7 us -> 69.6 us
    unnamed x22 -> x0, local copies, waits for them, and re-layouts: 8.81 us -> none
    pallas_call x1, Pallas kernels: 4.38 us -> 2.44 us  [per_device(): pl.pallas_call(combine_kernel, out_shape=(jax.ShapeDtypeStruct((4, 4, 6,...]
where the time goes in v2:
time: 70.3 us; the launch traced here: 70.2 us
  Pallas kernels  69.6 us (99%)
    pallas_call x1, Pallas kernels, per_device(): pl.pallas_call(krylov_kernel, out_shape=kept, in_specs=[hbm_spec] * 4, ou...  67.1 us
    pallas_call x1, Pallas kernels, per_device(): pl.pallas_call(combine_kernel, out_shape=(jax.ShapeDtypeStruct((4, 4, 6,...  2.44 us

profile of v2, /device:TPU:1, one launch (start us, length us, event | category | flops | bytes accessed | tf_op | source)
XLA Modules:
  0.0 70.2 jit_solution(972004923724362052)
XLA Ops:
  0.6 67.1 %krylov.1 = (f32[3,4,16,24,256]{4,3,2,1,0:T(8,128)S(1)}, f32[4,6,16,256]{3,2,1,0:T(8,128)S(1)}, f32[3,3,8,24,256]{4,3,2,1,0:T(8,128)S(1)}, f32[3,12,24,256]{3,2,1,0:T(8,128)S(1)}, f32[8,128]{1,0:T(8,128)S(1)}) custom-call(f32[4,6,16,256]{3,2,1,0:T(8,128)} %start.1, f32[3,6,16,256]{3,2,1,0:T(8,128)} %wind.1, f32[6,16,256]{2,1,0:T(8,128)} %reac.1, ...), custom_call_target="tpu_custom_call" | custom-call | tf_op jit(solution)/shard_map/krylov/pallas_call | solution.py:487
  67.8 2.4 %combine.1 = (f32[4,4,6,16,256]{4,3,2,1,0:T(8,128)}, f32[3,4,6,16,256]{4,3,2,1,0:T(8,128)}, f32[4,3]{1,0:T(4,128)}) custom-call(f32[3,4,16,24,256]{4,3,2,1,0:T(8,128)S(1)} %get-tuple-element.8.vec, f32[4,6,16,256]{3,2,1,0:T(8,128)S(1)} %get-tuple-element.9.w2, f32[3,3,8,24,256]{4,3,2,1,0:T(8,128)S(1)} %get-tuple-element.10.y1, ...), custom_call_target="tpu_custom_call" | custom-call | tf_op jit(solution)/shard_map/combine/pallas_call | solution.py:511

commit v3 on v2

--- a/solution.py
+++ b/solution.py
@@ -47,28 +47,27 @@
 def krylov_kernel(
     start, wind, reac, mass,
     vec, w2, y1, q, gram_out,
-    coef, work, t1, res, y0, part, slots_a, slots_b, slots_c,
+    coef, work, t1, res, y0, part, slots_a, slots_b,
     send_sems, recv_sems, load_sems,
 ):
     slab, sub = lax.axis_index("slab"), lax.axis_index("sub")
     slabs = lax.axis_size("slab")
     other = 1 - sub
-    x, y, z = lax.rem(slab, NX_T), lax.rem(lax.div(slab, NX_T), NY_T), lax.div(slab, NX_T * NY_T)
+    z = lax.div(slab, NX_T * NY_T)
     has_left, has_right = slab > 0, slab < slabs - 1
     left, right = jnp.maximum(slab - 1, 0), jnp.minimum(slab + 1, slabs - 1)
     own_rows = pl.ds(pl.multiple_of(8 * sub, 8), 16)
     out_tile = pl.ds(8, 8)
     in_tile = pl.ds(pl.multiple_of(16 * sub, 8), 8)
-    hbm_tile = pl.ds(pl.multiple_of(8 * other, 8), 8)
+
+    plane = 2 * NX_T * NY_T
+    in_plane = lax.rem(2 * slab + sub, plane)
 
     def peers(stage):
         if stage == 0:
-            for k in range(1, 2 * NX_T):
-                at = lax.rem(2 * x + sub + k, 2 * NX_T)
-                yield (slab - x + lax.div(at, 2), lax.rem(at, 2))
-        elif stage == 1:
-            for k in range(1, NY_T):
-                yield (slab + NX_T * (lax.rem(y + k, NY_T) - y), sub)
+            for k in range(1, plane):
+                at = lax.rem(in_plane + k, plane)
+                yield (z * (NX_T * NY_T) + lax.div(at, 2), lax.rem(at, 2))
         else:
             for k in range(1, NZ_T):
                 yield (slab + NX_T * NY_T * (lax.rem(z + k, NZ_T) - z), sub)
@@ -84,7 +83,7 @@
 
     barrier = pltpu.get_barrier_semaphore()
     count = 0
-    for stage in range(3):
+    for stage in range(2):
         for peer in peers(stage):
             pl.semaphore_signal(barrier, inc=1, device_id=peer, device_id_type=MESH_ID)
             count += 1
@@ -172,38 +171,30 @@
         def velocity(planes, rows):
             return vec.at[k, pl.ds(0, 3), planes, rows]
 
-        if k == 0:
-            p_src = (start.at[3, pl.ds(0, 5)], start.at[3, pl.ds(1, 5)], start.at[3, :, hbm_tile])
-            u_src = tuple(
-                start.at[pl.ds(0, 3), planes] for planes in (pl.ds(0, 2), pl.ds(4, 2))
-            ) + (start.at[pl.ds(0, 3), :, hbm_tile],)
-        else:
-            p_src = (
-                pressure(pl.ds(5, 5), own_rows), pressure(pl.ds(6, 5), own_rows),
-                pressure(pl.ds(5, 6), out_tile),
-            )
-            u_src = (
-                velocity(pl.ds(5, 2), own_rows), velocity(pl.ds(9, 2), own_rows),
-                velocity(pl.ds(5, 6), out_tile),
-            )
+        p_src = (
+            pressure(pl.ds(5, 5), own_rows), pressure(pl.ds(6, 5), own_rows),
+            pressure(pl.ds(5, 6), out_tile),
+        )
+        u_src = (
+            velocity(pl.ds(5, 2), own_rows), velocity(pl.ds(9, 2), own_rows),
+            velocity(pl.ds(5, 6), out_tile),
+        )
         p_halo = Halo(*p_src, pressure, pl.ds(0, 5), pl.ds(11, 5), pl.ds(5, 6))
         u_halo = Halo(*u_src, velocity, pl.ds(3, 2), pl.ds(11, 2), pl.ds(5, 6))
         return p_halo, u_halo
 
-    def coef_halo(src, buffer):
-        if len(src.shape) == 4:
-            parts = (src.at[:, pl.ds(0, 3)], src.at[:, pl.ds(3, 3)], src.at[:, :, hbm_tile])
-        else:
-            parts = (src.at[pl.ds(0, 3)], src.at[pl.ds(3, 3)], src.at[:, hbm_tile])
+    def coef_halo(buffer):
+        parts = (
+            buffer(pl.ds(3, 3), own_rows), buffer(pl.ds(6, 3), own_rows), buffer(pl.ds(3, 6), out_tile),
+        )
         return Halo(*parts, buffer, pl.ds(0, 3), pl.ds(9, 3), pl.ds(3, 6))
 
     p_halo, u_halo = vec_halo(0)
-    coef_halos = [
-        coef_halo(wind, lambda planes, rows: coef.at[pl.ds(0, 3), planes, rows]),
-        coef_halo(reac, lambda planes, rows: coef.at[3, planes, rows]),
-        coef_halo(mass, lambda planes, rows: coef.at[4, planes, rows]),
-    ]
+    coef_halos = [coef_halo(lambda planes, rows: coef.at[:, planes, rows])]
+    loads[0].wait()
     p_halo.send()
+    for copy in loads[1:]:
+        copy.wait()
     for halo in coef_halos:
         halo.send()
     u_halo.send()
@@ -265,16 +256,16 @@
             put(t1, [scale * (7.0 * a + b) for a, b in zip(f, total)], j)
             return 0
 
-        lax.fori_loop(1, 15, guess, 0)
+        lax.fori_loop(1, 15, guess, 0, unroll=7)
 
         def schur(j, _):
             value = transport(get(t1, j + 1), get(t1, j + 2), get(t1, j + 3), weights(j))
             put(q, [a * b for a, b in zip(value, get(work, 8, j))], k, j)
             return 0
 
-        lax.fori_loop(0, 12, schur, 0)
-
-    def velocity_part(k, target):
+        lax.fori_loop(0, 12, schur, 0, unroll=6)
+
+    def velocity_part(k, target, after_pressure=lambda: None):
         def first_guess(j, _):
             slope = gradient(get(q, k, j), get(q, k, j + 1), get(q, k, j + 2))
             inverse = get(work, 7, j + 1)
@@ -284,7 +275,7 @@
                 put(y0, [a * b for a, b in zip(r, inverse)], d, j)
             return 0
 
-        lax.fori_loop(0, 10, first_guess, 0)
+        lax.fori_loop(0, 10, first_guess, 0, unroll=5)
 
         def second_guess(j, _):
             w = weights(j + 2)
@@ -296,77 +287,82 @@
                 put(y1, [a + (b - c) * i for a, b, c, i in zip(f, r, value, inverse)], k, d, j)
             return 0
 
-        lax.fori_loop(0, 8, second_guess, 0)
+        lax.fori_loop(0, 8, second_guess, 0, unroll=4)
 
         def store(f, j, value):
             for i, h in enumerate(value):
                 mine = jnp.where(sub == 0, h[0:16], h[8:24])
                 target(f, j)[own_rows if k < 2 else slice(None), pl.ds(HALF * i, HALF)] = mine
 
-        def image(j, _):
+        def image_pressure(j, _):
+            pc = get(q, k, j + 3)
+            total = six(get(q, k, j + 2), pc, get(q, k, j + 4))
+            yc, zc = get(y1, k, 1, j + 1), get(y1, k, 2, j + 1)
+            ends = (
+                (get(y1, k, 0, j + 2), get(y1, k, 0, j)), (up_y(yc), down_y(yc)),
+                (up_z(zc, last), down_z(zc, first)),
+            )
+            flow = [a - b for a, b in zip(*ends[0])]
+            for high, low in ends[1:]:
+                flow = [t + (a - b) for t, a, b in zip(flow, high, low)]
+            store(3, j, [-0.5 * (a + (6.0 * b - c)) for a, b, c in zip(flow, pc, total)])
+            return 0
+
+        lax.fori_loop(0, 6, image_pressure, 0, unroll=6)
+        after_pressure()
+
+        def image_velocity(j, _):
             w = weights(j + 3)
-            pm, pc, pp = get(q, k, j + 2), get(q, k, j + 3), get(q, k, j + 4)
-            slope = gradient(pm, pc, pp)
-            flow = None
+            slope = gradient(get(q, k, j + 2), get(q, k, j + 3), get(q, k, j + 4))
             for d in range(3):
-                fm, f, fp = get(y1, k, d, j), get(y1, k, d, j + 1), get(y1, k, d, j + 2)
-                value = transport(fm, f, fp, w)
+                value = transport(get(y1, k, d, j), get(y1, k, d, j + 1), get(y1, k, d, j + 2), w)
                 store(d, j, [a + b for a, b in zip(value, slope[d])])
-                ends = ((fp, fm), (up_y(f), down_y(f)), (up_z(f, last), down_z(f, first)))[d]
-                part_flow = [a - b for a, b in zip(*ends)]
-                flow = part_flow if flow is None else [a + b for a, b in zip(flow, part_flow)]
-            total = six(pm, pc, pp)
-            store(3, j, [-0.5 * (a + (6.0 * b - c)) for a, b, c in zip(flow, pc, total)])
-            return 0
-
-        lax.fori_loop(0, 6, image, 0)
+            return 0
+
+        lax.fori_loop(0, 6, image_velocity, 0, unroll=3)
 
     lane8 = lax.broadcasted_iota(jnp.int32, (8, HALF), 1)
 
     def vectors(i, f, j):
-        if i < 3:
-            block = vec[i, f, 5 + j, own_rows, :]
-        else:
-            block = w2[f, j]
-        return block
+        return vec[i, f, 5 + j, own_rows, :] if i < 3 else w2[f, j]
 
     def dots(new, olds):
-        def step(i, accs):
-            f, j = lax.div(i, 6), lax.rem(i, 6)
-            b = vectors(new, f, j)
-            out = []
-            for acc, old in zip(accs, olds):
-                prod = b * (b if old == new else vectors(old, f, j))
-                out.append(acc + ((prod[0:8, 0:HALF] + prod[0:8, HALF:]) + (prod[8:16, 0:HALF] + prod[8:16, HALF:])))
-            return tuple(out)
+        def step(j, accs):
+            accs = list(accs)
+            for f in range(4):
+                b = vectors(new, f, j)
+                for i, old in enumerate(olds):
+                    prod = b * (b if old == new else vectors(old, f, j))
+                    accs[i] = accs[i] + (
+                        (prod[0:8, 0:HALF] + prod[0:8, HALF:]) + (prod[8:16, 0:HALF] + prod[8:16, HALF:])
+                    )
+            return tuple(accs)
 
         zero = jnp.zeros((8, HALF), jnp.float32)
-        return lax.fori_loop(0, 24, step, tuple(zero for _ in olds))
+        return lax.fori_loop(0, 6, step, tuple(zero for _ in olds), unroll=2)
 
     def pack(total, sums, at):
         for i, s in enumerate(sums):
             total = jnp.where(lane8 == at + i, jnp.sum(s, axis=1, keepdims=True), total)
         return total
 
-    for copy in loads:
-        copy.wait()
     p_halo.forward()
     for halo in coef_halos:
         halo.forward()
     p_halo.finish()
     for halo in coef_halos:
         halo.finish()
-    lax.fori_loop(0, 12, prepare, 0)
+    lax.fori_loop(0, 12, prepare, 0, unroll=2)
     pressure_part(0)
     u_halo.forward()
     u_halo.finish()
-    velocity_part(0, lambda f, j: vec.at[1, f, 5 + j])
+    halos = [vec_halo(1), vec_halo(2)]
+    velocity_part(0, lambda f, j: vec.at[1, f, 5 + j], halos[0][0].send)
 
     gram = jnp.zeros((8, HALF), jnp.float32)
     at = 0
     for k in range(2):
-        p_halo, u_halo = vec_halo(k + 1)
-        p_halo.send()
+        p_halo, u_halo = halos[k]
         u_halo.send()
         if k == 0:
             gram = pack(gram, dots(0, (0,)), 0)
@@ -379,23 +375,23 @@
         pressure_part(k + 1)
         u_halo.forward()
         u_halo.finish()
-        velocity_part(k + 1, (lambda f, j: vec.at[2, f, 5 + j]) if k == 0 else (lambda f, j: w2.at[f, j]))
+        if k == 0:
+            velocity_part(1, lambda f, j: vec.at[2, f, 5 + j], halos[1][0].send)
+        else:
+            velocity_part(2, lambda f, j: w2.at[f, j])
     gram = pack(gram, dots(3, (0, 1, 2, 3)), at)
 
-    places = (2 * x + sub, y, z)
-    for stage, slots in enumerate((slots_a, slots_b, slots_c)):
-        place = places[stage]
-        part[stage] = gram
-        slots[place] = gram
+    row_sum = jnp.sum(gram, axis=0, keepdims=True)
+    for stage, (place, slots) in enumerate(((in_plane, slots_a), (z, slots_b))):
+        part[stage] = row_sum
+        slots[place] = row_sum
         copies = [remote(part.at[stage], slots.at[place], peer) for peer in peers(stage)]
         for copy in copies:
             go(copy)
         for copy in copies:
             arrive(copy)
-        gram = slots[0]
-        for i in range(1, slots.shape[0]):
-            gram = gram + slots[i]
-    gram_out[...] = gram
+        row_sum = jnp.sum(slots[...], axis=0)
+    gram_out[...] = row_sum
 
     for copy, condition in started:
         if condition is None:
@@ -407,7 +403,7 @@
 def combine_kernel(vec, w2, y1, q, gram, basis, search, hess, b_out, s_out, out_sems):
     own_rows = pl.ds(pl.multiple_of(8 * lax.axis_index("sub"), 8), 16)
 
-    total = jnp.sum(gram[...], axis=0, keepdims=True)
+    total = gram[...]
     lane = lax.broadcasted_iota(jnp.int32, (1, HALF), 1)
 
     def entry(i):
@@ -475,13 +471,13 @@
     f32 = jnp.float32
     hbm_spec = pl.BlockSpec(memory_space=pltpu.HBM)
     vmem_spec = pl.BlockSpec(memory_space=pltpu.VMEM)
-    n_remote = 10 * 3 + 15 + 7 + 3 + 7
+    n_remote = 10 * 3 + 5 + 2 * NX_T * NY_T + NZ_T
     kept = (
         jax.ShapeDtypeStruct((3, 4, 16, ROWS, 256), f32),
         jax.ShapeDtypeStruct((4, 6, 16, 256), f32),
         jax.ShapeDtypeStruct((3, 3, 8, ROWS, 256), f32),
         jax.ShapeDtypeStruct((3, 12, ROWS, 256), f32),
-        jax.ShapeDtypeStruct((8, HALF), f32),
+        jax.ShapeDtypeStruct((1, HALF), f32),
     )
     arrays = [pltpu.with_memory_space_constraint(a, pltpu.HBM) for a in (start, wind, reaction, mass)]
     outs = pl.pallas_call(
@@ -495,10 +491,9 @@
             pltpu.VMEM((16, ROWS, 256), f32),
             pltpu.VMEM((3, 10, ROWS, 256), f32),
             pltpu.VMEM((3, 10, ROWS, 256), f32),
-            pltpu.VMEM((3, 8, HALF), f32),
-            pltpu.VMEM((8, 8, HALF), f32),
-            pltpu.VMEM((4, 8, HALF), f32),
-            pltpu.VMEM((8, 8, HALF), f32),
+            pltpu.VMEM((2, 1, HALF), f32),
+            pltpu.VMEM((2 * NX_T * NY_T, 1, HALF), f32),
+            pltpu.VMEM((NZ_T, 1, HALF), f32),
             pltpu.SemaphoreType.DMA((n_remote,)),
             pltpu.SemaphoreType.DMA((n_remote,)),
             pltpu.SemaphoreType.DMA((4,)),

time: 70.3 us -> 60.7 us (0.86)
  Pallas kernels: 69.6 us -> 59.9 us
    pallas_call x1, Pallas kernels: 67.1 us -> 57.5 us  [per_device(): pl.pallas_call(krylov_kernel, out_shape=kept, in_specs=[hbm_spec] * 4, ou...]
where the time goes in v3:
time: 60.7 us; the launch traced here: 60.6 us
  Pallas kernels  59.9 us (99%)
  between operations  0.64 us (1%)
    pallas_call x1, Pallas kernels, per_device(): pl.pallas_call(krylov_kernel, out_shape=kept, in_specs=[hbm_spec] * 4, ou...  57.5 us
    pallas_call x1, Pallas kernels, per_device(): pl.pallas_call(combine_kernel, out_shape=(jax.ShapeDtypeStruct((4, 4, 6,...  2.43 us

profile of v3, /device:TPU:1, one launch (start us, length us, event | category | flops | bytes accessed | tf_op | source)
XLA Modules:
  0.0 60.6 jit_solution(6310651461231323863)
XLA Ops:
  0.6 57.5 %krylov.1 = (f32[3,4,16,24,256]{4,3,2,1,0:T(8,128)S(1)}, f32[4,6,16,256]{3,2,1,0:T(8,128)S(1)}, f32[3,3,8,24,256]{4,3,2,1,0:T(8,128)S(1)}, f32[3,12,24,256]{3,2,1,0:T(8,128)S(1)}, f32[1,128]{1,0:T(1,128)S(1)}) custom-call(f32[4,6,16,256]{3,2,1,0:T(8,128)} %start.1, f32[3,6,16,256]{3,2,1,0:T(8,128)} %wind.1, f32[6,16,256]{2,1,0:T(8,128)} %reac.1, ...), custom_call_target="tpu_custom_call" | custom-call | tf_op jit(solution)/shard_map/krylov/pallas_call | solution.py:483
  58.2 2.4 %combine.1 = (f32[4,4,6,16,256]{4,3,2,1,0:T(8,128)}, f32[3,4,6,16,256]{4,3,2,1,0:T(8,128)}, f32[4,3]{1,0:T(4,128)}) custom-call(f32[3,4,16,24,256]{4,3,2,1,0:T(8,128)S(1)} %get-tuple-element.8.vec, f32[4,6,16,256]{3,2,1,0:T(8,128)S(1)} %get-tuple-element.9.w2, f32[3,3,8,24,256]{4,3,2,1,0:T(8,128)S(1)} %get-tuple-element.10.y1, ...), custom_call_target="tpu_custom_call" | custom-call | tf_op jit(solution)/shard_map/combine/pallas_call | solution.py:506

commit v4 on v3

--- a/solution.py
+++ b/solution.py
@@ -96,6 +96,12 @@
     def _():
         pl.semaphore_signal(barrier, inc=1, device_id=(right, sub), device_id_type=MESH_ID)
 
+    halo_rows = pl.ds(pl.multiple_of(16 * other, 8), 8)
+    for k in range(3):
+        for d in range(3):
+            for plane_at in (3, 12):
+                vec[k, d, plane_at, halo_rows] = jnp.zeros((8, 256), jnp.float32)
+
     def clear(planes, coef_planes):
         for k in range(3):
             for f in range(4):
@@ -164,6 +170,18 @@
             arrive(self.low_on, has_left)
             arrive(self.high_on, has_right)
 
+    class FarHalo:
+        def __init__(self, to_right, to_left):
+            self.to_right, self.to_left = to_right, to_left
+
+        def send(self):
+            go(self.to_right, has_right)
+            go(self.to_left, has_left)
+
+        def finish(self):
+            arrive(self.to_right, has_left)
+            arrive(self.to_left, has_right)
+
     def vec_halo(k):
         def pressure(planes, rows):
             return vec.at[k, 3, planes, rows]
@@ -175,13 +193,17 @@
             pressure(pl.ds(5, 5), own_rows), pressure(pl.ds(6, 5), own_rows),
             pressure(pl.ds(5, 6), out_tile),
         )
-        u_src = (
-            velocity(pl.ds(5, 2), own_rows), velocity(pl.ds(9, 2), own_rows),
+        near_src = (
+            velocity(pl.ds(5, 1), own_rows), velocity(pl.ds(10, 1), own_rows),
             velocity(pl.ds(5, 6), out_tile),
         )
         p_halo = Halo(*p_src, pressure, pl.ds(0, 5), pl.ds(11, 5), pl.ds(5, 6))
-        u_halo = Halo(*u_src, velocity, pl.ds(3, 2), pl.ds(11, 2), pl.ds(5, 6))
-        return p_halo, u_halo
+        near = Halo(*near_src, velocity, pl.ds(4, 1), pl.ds(11, 1), pl.ds(5, 6))
+        far = FarHalo(
+            remote(velocity(pl.ds(9, 1), own_rows), velocity(pl.ds(3, 1), own_rows), (right, sub)),
+            remote(velocity(pl.ds(6, 1), own_rows), velocity(pl.ds(12, 1), own_rows), (left, sub)),
+        )
+        return p_halo, near, far
 
     def coef_halo(buffer):
         parts = (
@@ -189,7 +211,7 @@
         )
         return Halo(*parts, buffer, pl.ds(0, 3), pl.ds(9, 3), pl.ds(3, 6))
 
-    p_halo, u_halo = vec_halo(0)
+    p_halo, near, far = vec_halo(0)
     coef_halos = [coef_halo(lambda planes, rows: coef.at[:, planes, rows])]
     loads[0].wait()
     p_halo.send()
@@ -197,7 +219,8 @@
         copy.wait()
     for halo in coef_halos:
         halo.send()
-    u_halo.send()
+    near.send()
+    far.send()
 
     last, first = lane_is(HALF - 1), lane_is(0)
     row = lax.broadcasted_iota(jnp.int32, (ROWS, HALF), 0)
@@ -352,18 +375,20 @@
     p_halo.finish()
     for halo in coef_halos:
         halo.finish()
+    near.forward()
     lax.fori_loop(0, 12, prepare, 0, unroll=2)
     pressure_part(0)
-    u_halo.forward()
-    u_halo.finish()
+    near.finish()
+    far.finish()
     halos = [vec_halo(1), vec_halo(2)]
     velocity_part(0, lambda f, j: vec.at[1, f, 5 + j], halos[0][0].send)
 
     gram = jnp.zeros((8, HALF), jnp.float32)
     at = 0
     for k in range(2):
-        p_halo, u_halo = halos[k]
-        u_halo.send()
+        p_halo, near, far = halos[k]
+        near.send()
+        far.send()
         if k == 0:
             gram = pack(gram, dots(0, (0,)), 0)
             at = 1
@@ -372,9 +397,10 @@
         at += len(olds)
         p_halo.forward()
         p_halo.finish()
+        near.forward()
         pressure_part(k + 1)
-        u_halo.forward()
-        u_halo.finish()
+        near.finish()
+        far.finish()
         if k == 0:
             velocity_part(1, lambda f, j: vec.at[2, f, 5 + j], halos[1][0].send)
         else:
@@ -458,7 +484,7 @@
                     done.append(value)
             return 0
 
-        lax.fori_loop(0, 6, body, 0)
+        lax.fori_loop(0, 6, body, 0, unroll=3)
         for i, (src, dst) in enumerate(((b_out, basis), (s_out, search))):
             copy = pltpu.make_async_copy(src.at[:, f], dst.at[:, f], out_sems.at[f, i])
             copy.start()
@@ -471,7 +497,7 @@
     f32 = jnp.float32
     hbm_spec = pl.BlockSpec(memory_space=pltpu.HBM)
     vmem_spec = pl.BlockSpec(memory_space=pltpu.VMEM)
-    n_remote = 10 * 3 + 5 + 2 * NX_T * NY_T + NZ_T
+    n_remote = 12 * 3 + 5 + 2 * NX_T * NY_T + NZ_T
     kept = (
         jax.ShapeDtypeStruct((3, 4, 16, ROWS, 256), f32),
         jax.ShapeDtypeStruct((4, 6, 16, 256), f32),

time: 60.7 us -> 58.4 us (0.962)
  Pallas kernels: 59.9 us -> 57.7 us
    pallas_call x1, Pallas kernels: 57.5 us -> 55.3 us  [per_device(): pl.pallas_call(krylov_kernel, out_shape=kept, in_specs=[hbm_spec] * 4, ou...]
where the time goes in v4:
time: 58.4 us; the launch traced here: 58.3 us
  Pallas kernels  57.7 us (99%)
  between operations  0.64 us (1%)
    pallas_call x1, Pallas kernels, per_device(): pl.pallas_call(krylov_kernel, out_shape=kept, in_specs=[hbm_spec] * 4, ou...  55.3 us
    pallas_call x1, Pallas kernels, per_device(): pl.pallas_call(combine_kernel, out_shape=(jax.ShapeDtypeStruct((4, 4, 6,...  2.41 us

profile of v4, /device:TPU:1, one launch (start us, length us, event | category | flops | bytes accessed | tf_op | source)
XLA Modules:
  0.0 58.3 jit_solution(13260699776200477774)
XLA Ops:
  0.6 55.3 %krylov.1 = (f32[3,4,16,24,256]{4,3,2,1,0:T(8,128)S(1)}, f32[4,6,16,256]{3,2,1,0:T(8,128)S(1)}, f32[3,3,8,24,256]{4,3,2,1,0:T(8,128)S(1)}, f32[3,12,24,256]{3,2,1,0:T(8,128)S(1)}, f32[1,128]{1,0:T(1,128)S(1)}) custom-call(f32[4,6,16,256]{3,2,1,0:T(8,128)} %start.1, f32[3,6,16,256]{3,2,1,0:T(8,128)} %wind.1, f32[6,16,256]{2,1,0:T(8,128)} %reac.1, ...), custom_call_target="tpu_custom_call" | custom-call | tf_op jit(solution)/shard_map/krylov/pallas_call | solution.py:509
  55.9 2.4 %combine.1 = (f32[4,4,6,16,256]{4,3,2,1,0:T(8,128)}, f32[3,4,6,16,256]{4,3,2,1,0:T(8,128)}, f32[4,3]{1,0:T(4,128)}) custom-call(f32[3,4,16,24,256]{4,3,2,1,0:T(8,128)S(1)} %get-tuple-element.8.vec, f32[4,6,16,256]{3,2,1,0:T(8,128)S(1)} %get-tuple-element.9.w2, f32[3,3,8,24,256]{4,3,2,1,0:T(8,128)S(1)} %get-tuple-element.10.y1, ...), custom_call_target="tpu_custom_call" | custom-call | tf_op jit(solution)/shard_map/combine/pallas_call | solution.py:532

commit v5 on v4

--- a/solution.py
+++ b/solution.py
@@ -74,9 +74,9 @@
 
     loads = [
         pltpu.make_async_copy(start, vec.at[0, :, pl.ds(5, 6), own_rows], load_sems.at[0]),
-        pltpu.make_async_copy(wind, coef.at[pl.ds(0, 3), pl.ds(3, 6), own_rows], load_sems.at[1]),
-        pltpu.make_async_copy(reac, coef.at[3, pl.ds(3, 6), own_rows], load_sems.at[2]),
-        pltpu.make_async_copy(mass, coef.at[4, pl.ds(3, 6), own_rows], load_sems.at[3]),
+        pltpu.make_async_copy(wind, coef.at[pl.ds(0, 3), pl.ds(2, 6), own_rows], load_sems.at[1]),
+        pltpu.make_async_copy(reac, coef.at[3, pl.ds(2, 6), own_rows], load_sems.at[2]),
+        pltpu.make_async_copy(mass, coef.at[4, pl.ds(2, 6), own_rows], load_sems.at[3]),
     ]
     for copy in loads:
         copy.start()
@@ -101,21 +101,25 @@
         for d in range(3):
             for plane_at in (3, 12):
                 vec[k, d, plane_at, halo_rows] = jnp.zeros((8, 256), jnp.float32)
-
-    def clear(planes, coef_planes):
+        for plane_at in (0, 11):
+            q[k, plane_at, halo_rows] = jnp.zeros((8, 256), jnp.float32)
+
+    def clear(planes, coef_planes, far_plane):
         for k in range(3):
             for f in range(4):
                 vec[k, f, planes] = jnp.zeros((5, ROWS, 256), jnp.float32)
         for f in range(5):
-            coef[f, coef_planes] = jnp.zeros((3, ROWS, 256), jnp.float32)
+            coef[f, coef_planes] = jnp.zeros((2, ROWS, 256), jnp.float32)
+        for k in range(3):
+            q[k, far_plane] = jnp.zeros((ROWS, 256), jnp.float32)
 
     @pl.when(jnp.logical_not(has_left))
     def _():
-        clear(pl.ds(0, 5), pl.ds(0, 3))
+        clear(pl.ds(0, 5), pl.ds(0, 2), 0)
 
     @pl.when(jnp.logical_not(has_right))
     def _():
-        clear(pl.ds(11, 5), pl.ds(9, 3))
+        clear(pl.ds(11, 5), pl.ds(8, 2), 11)
 
     pl.semaphore_wait(
         barrier, count + has_left.astype(jnp.int32) + has_right.astype(jnp.int32)
@@ -166,7 +170,6 @@
             go(self.high_on, has_right)
 
         def finish(self):
-            arrive(self.to_other)
             arrive(self.low_on, has_left)
             arrive(self.high_on, has_right)
 
@@ -190,37 +193,40 @@
             return vec.at[k, pl.ds(0, 3), planes, rows]
 
         p_src = (
-            pressure(pl.ds(5, 5), own_rows), pressure(pl.ds(6, 5), own_rows),
+            pressure(pl.ds(5, 4), own_rows), pressure(pl.ds(7, 4), own_rows),
             pressure(pl.ds(5, 6), out_tile),
         )
         near_src = (
             velocity(pl.ds(5, 1), own_rows), velocity(pl.ds(10, 1), own_rows),
             velocity(pl.ds(5, 6), out_tile),
         )
-        p_halo = Halo(*p_src, pressure, pl.ds(0, 5), pl.ds(11, 5), pl.ds(5, 6))
+        p_halo = Halo(*p_src, pressure, pl.ds(1, 4), pl.ds(11, 4), pl.ds(5, 6))
         near = Halo(*near_src, velocity, pl.ds(4, 1), pl.ds(11, 1), pl.ds(5, 6))
         far = FarHalo(
             remote(velocity(pl.ds(9, 1), own_rows), velocity(pl.ds(3, 1), own_rows), (right, sub)),
             remote(velocity(pl.ds(6, 1), own_rows), velocity(pl.ds(12, 1), own_rows), (left, sub)),
         )
-        return p_halo, near, far
+        schur_far = FarHalo(
+            remote(q.at[k, 6, own_rows], q.at[k, 0, own_rows], (right, sub)),
+            remote(q.at[k, 5, own_rows], q.at[k, 11, own_rows], (left, sub)),
+        )
+        return p_halo, near, far, schur_far
 
     def coef_halo(buffer):
         parts = (
-            buffer(pl.ds(3, 3), own_rows), buffer(pl.ds(6, 3), own_rows), buffer(pl.ds(3, 6), out_tile),
-        )
-        return Halo(*parts, buffer, pl.ds(0, 3), pl.ds(9, 3), pl.ds(3, 6))
-
-    p_halo, near, far = vec_halo(0)
-    coef_halos = [coef_halo(lambda planes, rows: coef.at[:, planes, rows])]
+            buffer(pl.ds(2, 2), own_rows), buffer(pl.ds(6, 2), own_rows), buffer(pl.ds(2, 6), out_tile),
+        )
+        return Halo(*parts, buffer, pl.ds(0, 2), pl.ds(8, 2), pl.ds(2, 6))
+
+    halos = [vec_halo(k) for k in range(3)]
+    coef_halo = coef_halo(lambda planes, rows: coef.at[:, planes, rows])
     loads[0].wait()
-    p_halo.send()
+    halos[0][0].send()
     for copy in loads[1:]:
         copy.wait()
-    for halo in coef_halos:
+    coef_halo.send()
+    for halo in halos[0][1:3]:
         halo.send()
-    near.send()
-    far.send()
 
     last, first = lane_is(HALF - 1), lane_is(0)
     row = lax.broadcasted_iota(jnp.int32, (ROWS, HALF), 0)
@@ -231,7 +237,7 @@
         return jnp.logical_and(at >= 0, at < slabs * 6)
 
     def prepare(j, _):
-        ok = jnp.logical_and(live, inside(j + 2))
+        ok = jnp.logical_and(live, inside(j + 3))
         for d in range(3):
             half = [0.5 * h for h in get(coef, d, j)]
             put(work, [h - 1.0 for h in half], d, j)
@@ -268,49 +274,55 @@
             half_difference(up_z(f, last), down_z(f, first)),
         )
 
-    def pressure_part(k):
-        def masked(j):
-            return [jnp.where(live, h, 0.0) for h in get(vec, k, 3, j)]
-
-        def guess(j, _):
-            scale = jnp.where(jnp.logical_and(live, inside(j)), 1.0 / 49.0, 0.0)
-            f = masked(j)
-            total = six(get(vec, k, 3, j - 1), f, get(vec, k, 3, j + 1))
-            put(t1, [scale * (7.0 * a + b) for a, b in zip(f, total)], j)
+    def loop(count, body, plane, unroll):
+        def step(i, _):
+            body(plane(i))
             return 0
 
-        lax.fori_loop(1, 15, guess, 0, unroll=7)
-
-        def schur(j, _):
-            value = transport(get(t1, j + 1), get(t1, j + 2), get(t1, j + 3), weights(j))
-            put(q, [a * b for a, b in zip(value, get(work, 8, j))], k, j)
-            return 0
-
-        lax.fori_loop(0, 12, schur, 0, unroll=6)
-
-    def velocity_part(k, target, after_pressure=lambda: None):
-        def first_guess(j, _):
-            slope = gradient(get(q, k, j), get(q, k, j + 1), get(q, k, j + 2))
-            inverse = get(work, 7, j + 1)
-            for d in range(3):
-                r = [a - b for a, b in zip(get(vec, k, d, j + 3), slope[d])]
-                put(res, r, d, j)
-                put(y0, [a * b for a, b in zip(r, inverse)], d, j)
-            return 0
-
-        lax.fori_loop(0, 10, first_guess, 0, unroll=5)
-
-        def second_guess(j, _):
-            w = weights(j + 2)
-            inverse = get(work, 7, j + 2)
-            for d in range(3):
-                f = get(y0, d, j + 1)
-                value = transport(get(y0, d, j), f, get(y0, d, j + 2), w)
-                r = get(res, d, j + 1)
-                put(y1, [a + (b - c) * i for a, b, c, i in zip(f, r, value, inverse)], k, d, j)
-            return 0
-
-        lax.fori_loop(0, 8, second_guess, 0, unroll=4)
+        lax.fori_loop(0, count, step, 0, unroll=unroll)
+
+    def guess(k, j):
+        scale = jnp.where(jnp.logical_and(live, inside(j)), 1.0 / 49.0, 0.0)
+        f = [jnp.where(live, h, 0.0) for h in get(vec, k, 3, j)]
+        total = six(get(vec, k, 3, j - 1), f, get(vec, k, 3, j + 1))
+        put(t1, [scale * (7.0 * a + b) for a, b in zip(f, total)], j)
+
+    def schur(k, j):
+        value = transport(get(t1, j - 1), get(t1, j), get(t1, j + 1), weights(j - 3))
+        put(q, [a * b for a, b in zip(value, get(work, 8, j - 3))], k, j - 2)
+
+    def pressure_inner(k):
+        loop(4, functools.partial(guess, k), lambda i: i + 6, 4)
+        loop(2, functools.partial(schur, k), lambda i: i + 7, 2)
+
+    def pressure_outer(k):
+        loop(8, functools.partial(guess, k), lambda i: i + 2 + 4 * lax.div(i, 4), 4)
+        loop(8, functools.partial(schur, k), lambda i: i + 3 + 2 * lax.div(i, 4), 4)
+
+    def first_guess(k, j):
+        slope = gradient(get(q, k, j), get(q, k, j + 1), get(q, k, j + 2))
+        inverse = get(work, 7, j)
+        for d in range(3):
+            r = [a - b for a, b in zip(get(vec, k, d, j + 3), slope[d])]
+            put(res, r, d, j)
+            put(y0, [a * b for a, b in zip(r, inverse)], d, j)
+
+    def second_guess(k, j):
+        w = weights(j + 1)
+        inverse = get(work, 7, j + 1)
+        for d in range(3):
+            f = get(y0, d, j + 1)
+            value = transport(get(y0, d, j), f, get(y0, d, j + 2), w)
+            r = get(res, d, j + 1)
+            put(y1, [a + (b - c) * i for a, b, c, i in zip(f, r, value, inverse)], k, d, j)
+
+    def velocity_inner(k):
+        loop(8, functools.partial(first_guess, k), lambda i: i + 1, 4)
+        loop(6, functools.partial(second_guess, k), lambda i: i + 1, 3)
+
+    def velocity_outer(k, target, after_pressure=lambda: None):
+        loop(2, functools.partial(first_guess, k), lambda i: 9 * i, 2)
+        loop(2, functools.partial(second_guess, k), lambda i: 7 * i, 2)
 
         def store(f, j, value):
             for i, h in enumerate(value):
@@ -335,7 +347,7 @@
         after_pressure()
 
         def image_velocity(j, _):
-            w = weights(j + 3)
+            w = weights(j + 2)
             slope = gradient(get(q, k, j + 2), get(q, k, j + 3), get(q, k, j + 4))
             for d in range(3):
                 value = transport(get(y1, k, d, j), get(y1, k, d, j + 1), get(y1, k, d, j + 2), w)
@@ -369,42 +381,47 @@
             total = jnp.where(lane8 == at + i, jnp.sum(s, axis=1, keepdims=True), total)
         return total
 
-    p_halo.forward()
-    for halo in coef_halos:
-        halo.forward()
-    p_halo.finish()
-    for halo in coef_halos:
-        halo.finish()
-    near.forward()
-    lax.fori_loop(0, 12, prepare, 0, unroll=2)
-    pressure_part(0)
-    near.finish()
-    far.finish()
-    halos = [vec_halo(1), vec_halo(2)]
-    velocity_part(0, lambda f, j: vec.at[1, f, 5 + j], halos[0][0].send)
-
+    def application(k, target, after_pressure=lambda: None):
+        p_halo, near, far, schur_far = halos[k]
+        arrive(p_halo.to_other)
+        if k == 0:
+            arrive(coef_halo.to_other)
+            lax.fori_loop(2, 8, prepare, 0, unroll=2)
+        pressure_inner(k)
+        schur_far.send()
+        p_halo.forward()
+        if k == 0:
+            coef_halo.forward()
+        p_halo.finish()
+        near.forward()
+        if k == 0:
+            coef_halo.finish()
+            for planes in (0, 8):
+                lax.fori_loop(planes, planes + 2, prepare, 0, unroll=2)
+        pressure_outer(k)
+        arrive(near.to_other)
+        near.finish()
+        velocity_inner(k)
+        far.finish()
+        schur_far.finish()
+        velocity_outer(k, target, after_pressure)
+
+    application(0, lambda f, j: vec.at[1, f, 5 + j], halos[1][0].send)
     gram = jnp.zeros((8, HALF), jnp.float32)
     at = 0
     for k in range(2):
-        p_halo, near, far = halos[k]
-        near.send()
-        far.send()
+        halos[k + 1][1].send()
+        halos[k + 1][2].send()
         if k == 0:
             gram = pack(gram, dots(0, (0,)), 0)
             at = 1
         olds = tuple(range(k + 2))
         gram = pack(gram, dots(k + 1, olds), at)
         at += len(olds)
-        p_halo.forward()
-        p_halo.finish()
-        near.forward()
-        pressure_part(k + 1)
-        near.finish()
-        far.finish()
         if k == 0:
-            velocity_part(1, lambda f, j: vec.at[2, f, 5 + j], halos[1][0].send)
+            application(1, lambda f, j: vec.at[2, f, 5 + j], halos[2][0].send)
         else:
-            velocity_part(2, lambda f, j: w2.at[f, j])
+            application(2, lambda f, j: w2.at[f, j])
     gram = pack(gram, dots(3, (0, 1, 2, 3)), at)
 
     row_sum = jnp.sum(gram, axis=0, keepdims=True)
@@ -497,7 +514,7 @@
     f32 = jnp.float32
     hbm_spec = pl.BlockSpec(memory_space=pltpu.HBM)
     vmem_spec = pl.BlockSpec(memory_space=pltpu.VMEM)
-    n_remote = 12 * 3 + 5 + 2 * NX_T * NY_T + NZ_T
+    n_remote = 14 * 3 + 5 + 2 * NX_T * NY_T + NZ_T
     kept = (
         jax.ShapeDtypeStruct((3, 4, 16, ROWS, 256), f32),
         jax.ShapeDtypeStruct((4, 6, 16, 256), f32),
@@ -512,8 +529,8 @@
         in_specs=[hbm_spec] * 4,
         out_specs=(vmem_spec,) * 5,
         scratch_shapes=[
-            pltpu.VMEM((5, 12, ROWS, 256), f32),
-            pltpu.VMEM((9, 12, ROWS, 256), f32),
+            pltpu.VMEM((5, 10, ROWS, 256), f32),
+            pltpu.VMEM((9, 10, ROWS, 256), f32),
             pltpu.VMEM((16, ROWS, 256), f32),
             pltpu.VMEM((3, 10, ROWS, 256), f32),
             pltpu.VMEM((3, 10, ROWS, 256), f32),

time: 58.4 us -> 55.4 us (0.949)
  Pallas kernels: 57.7 us -> 54.7 us
    pallas_call x1, Pallas kernels: 55.3 us -> 52.3 us  [per_device(): pl.pallas_call(krylov_kernel, out_shape=kept, in_specs=[hbm_spec] * 4, ou...]
where the time goes in v5:
time: 55.4 us; the launch traced here: 55.3 us
  Pallas kernels  54.7 us (99%)
  between operations  0.64 us (1%)
    pallas_call x1, Pallas kernels, per_device(): pl.pallas_call(krylov_kernel, out_shape=kept, in_specs=[hbm_spec] * 4, ou...  52.3 us
    pallas_call x1, Pallas kernels, per_device(): pl.pallas_call(combine_kernel, out_shape=(jax.ShapeDtypeStruct((4, 4, 6,...  2.41 us

profile of v5, /device:TPU:1, one launch (start us, length us, event | category | flops | bytes accessed | tf_op | source)
XLA Modules:
  0.0 55.3 jit_solution(1829755746751671110)
XLA Ops:
  0.6 52.3 %krylov.1 = (f32[3,4,16,24,256]{4,3,2,1,0:T(8,128)S(1)}, f32[4,6,16,256]{3,2,1,0:T(8,128)S(1)}, f32[3,3,8,24,256]{4,3,2,1,0:T(8,128)S(1)}, f32[3,12,24,256]{3,2,1,0:T(8,128)S(1)}, f32[1,128]{1,0:T(1,128)S(1)}) custom-call(f32[4,6,16,256]{3,2,1,0:T(8,128)} %start.1, f32[3,6,16,256]{3,2,1,0:T(8,128)} %wind.1, f32[6,16,256]{2,1,0:T(8,128)} %reac.1, ...), custom_call_target="tpu_custom_call" | custom-call | tf_op jit(solution)/shard_map/krylov/pallas_call | solution.py:526
  52.9 2.4 %combine.1 = (f32[4,4,6,16,256]{4,3,2,1,0:T(8,128)}, f32[3,4,6,16,256]{4,3,2,1,0:T(8,128)}, f32[4,3]{1,0:T(4,128)}) custom-call(f32[3,4,16,24,256]{4,3,2,1,0:T(8,128)S(1)} %get-tuple-element.8.vec, f32[4,6,16,256]{3,2,1,0:T(8,128)S(1)} %get-tuple-element.9.w2, f32[3,3,8,24,256]{4,3,2,1,0:T(8,128)S(1)} %get-tuple-element.10.y1, ...), custom_call_target="tpu_custom_call" | custom-call | tf_op jit(solution)/shard_map/combine/pallas_call | solution.py:549

commit v6 on v5

--- a/solution.py
+++ b/solution.py
@@ -48,7 +48,7 @@
     start, wind, reac, mass,
     vec, w2, y1, q, gram_out,
     coef, work, t1, res, y0, part, slots_a, slots_b,
-    send_sems, recv_sems, load_sems,
+    send_sems, recv_sems, load_sems, told,
 ):
     slab, sub = lax.axis_index("slab"), lax.axis_index("sub")
     slabs = lax.axis_size("slab")
@@ -81,12 +81,34 @@
     for copy in loads:
         copy.start()
 
+    x, y = lax.rem(slab, NX_T), lax.rem(lax.div(slab, NX_T), NY_T)
+
+    def line_x():
+        for k in range(1, 2 * NX_T):
+            at = lax.rem(2 * x + sub + k, 2 * NX_T)
+            yield (slab - x + lax.div(at, 2), lax.rem(at, 2))
+
+    def line_y():
+        for k in range(1, NY_T):
+            yield (slab + NX_T * (lax.rem(y + k, NY_T) - y), sub)
+
+    def near_z():
+        for k in (1, NZ_T - 1):
+            yield (slab + NX_T * NY_T * (lax.rem(z + k, NZ_T) - z), sub)
+
+    def signal_all(sem, devices):
+        for device in devices:
+            pl.semaphore_signal(sem, inc=1, device_id=device, device_id_type=MESH_ID)
+        return len(devices)
+
+    def tell(turn):
+        return signal_all(told.at[turn], [*line_y(), *near_z()] if turn == 0 else [*near_z()])
+
+    def hear(turn, count):
+        pl.semaphore_wait(told.at[turn], count)
+
     barrier = pltpu.get_barrier_semaphore()
-    count = 0
-    for stage in range(2):
-        for peer in peers(stage):
-            pl.semaphore_signal(barrier, inc=1, device_id=peer, device_id_type=MESH_ID)
-            count += 1
+    count = signal_all(barrier, [*line_x(), *line_y(), *near_z()])
 
     @pl.when(has_left)
     def _():
@@ -124,6 +146,7 @@
     pl.semaphore_wait(
         barrier, count + has_left.astype(jnp.int32) + has_right.astype(jnp.int32)
     )
+    expected = tell(0)
 
     used = [0]
 
@@ -412,6 +435,8 @@
     for k in range(2):
         halos[k + 1][1].send()
         halos[k + 1][2].send()
+        hear(k, expected)
+        expected = tell(k + 1)
         if k == 0:
             gram = pack(gram, dots(0, (0,)), 0)
             at = 1
@@ -422,6 +447,7 @@
             application(1, lambda f, j: vec.at[2, f, 5 + j], halos[2][0].send)
         else:
             application(2, lambda f, j: w2.at[f, j])
+    hear(2, expected)
     gram = pack(gram, dots(3, (0, 1, 2, 3)), at)
 
     row_sum = jnp.sum(gram, axis=0, keepdims=True)
@@ -540,6 +566,7 @@
             pltpu.SemaphoreType.DMA((n_remote,)),
             pltpu.SemaphoreType.DMA((n_remote,)),
             pltpu.SemaphoreType.DMA((4,)),
+            pltpu.SemaphoreType.REGULAR((3,)),
         ],
         compiler_params=pltpu.CompilerParams(
             collective_id=0, has_side_effects=True, vmem_limit_bytes=24 * 2**20

time: 55.4 us -> 54.3 us (0.980)
  Pallas kernels: 54.7 us -> 53.5 us
    pallas_call x1, Pallas kernels: 52.3 us -> 51.1 us  [per_device(): pl.pallas_call(krylov_kernel, out_shape=kept, in_specs=[hbm_spec] * 4, ou...]
where the time goes in v6:
time: 54.3 us; the launch traced here: 54.2 us
  Pallas kernels  53.5 us (99%)
  between operations  0.64 us (1%)
    pallas_call x1, Pallas kernels, per_device(): pl.pallas_call(krylov_kernel, out_shape=kept, in_specs=[hbm_spec] * 4, ou...  51.1 us
    pallas_call x1, Pallas kernels, per_device(): pl.pallas_call(combine_kernel, out_shape=(jax.ShapeDtypeStruct((4, 4, 6,...  2.41 us

profile of v6, /device:TPU:1, one launch (start us, length us, event | category | flops | bytes accessed | tf_op | source)
XLA Modules:
  0.0 54.2 jit_solution(2946335399910978333)
XLA Ops:
  0.6 51.1 %krylov.1 = (f32[3,4,16,24,256]{4,3,2,1,0:T(8,128)S(1)}, f32[4,6,16,256]{3,2,1,0:T(8,128)S(1)}, f32[3,3,8,24,256]{4,3,2,1,0:T(8,128)S(1)}, f32[3,12,24,256]{3,2,1,0:T(8,128)S(1)}, f32[1,128]{1,0:T(1,128)S(1)}) custom-call(f32[4,6,16,256]{3,2,1,0:T(8,128)} %start.1, f32[3,6,16,256]{3,2,1,0:T(8,128)} %wind.1, f32[6,16,256]{2,1,0:T(8,128)} %reac.1, ...), custom_call_target="tpu_custom_call" | custom-call | tf_op jit(solution)/shard_map/krylov/pallas_call | solution.py:552
  51.8 2.4 %combine.1 = (f32[4,4,6,16,256]{4,3,2,1,0:T(8,128)}, f32[3,4,6,16,256]{4,3,2,1,0:T(8,128)}, f32[4,3]{1,0:T(4,128)}) custom-call(f32[3,4,16,24,256]{4,3,2,1,0:T(8,128)S(1)} %get-tuple-element.8.vec, f32[4,6,16,256]{3,2,1,0:T(8,128)S(1)} %get-tuple-element.9.w2, f32[3,3,8,24,256]{4,3,2,1,0:T(8,128)S(1)} %get-tuple-element.10.y1, ...), custom_call_target="tpu_custom_call" | custom-call | tf_op jit(solution)/shard_map/combine/pallas_call | solution.py:576

commit v7 on v6

--- a/solution.py
+++ b/solution.py
@@ -148,20 +148,33 @@
     )
     expected = tell(0)
 
-    used = [0]
+    used = {"send": 0, "receive": 0}
 
     def remote(src, dst, device):
-        at = used[0]
-        used[0] += 1
-        return pltpu.make_async_remote_copy(
-            src_ref=src, dst_ref=dst, send_sem=send_sems.at[at], recv_sem=recv_sems.at[at],
-            device_id=device, device_id_type=MESH_ID,
+        copy = pltpu.make_async_remote_copy(
+            src_ref=src, dst_ref=dst, send_sem=send_sems.at[used["send"]],
+            recv_sem=recv_sems.at[used["receive"]], device_id=device, device_id_type=MESH_ID,
         )
-
-    started = []
+        slot_of[id(copy)] = used["send"]
+        keep.append(copy)
+        used["send"] += 1
+        used["receive"] += 1
+        return copy
+
+    slot_of, keep, sending = {}, [], {}
+
+    def sent(slot):
+        copy, condition = sending.pop(slot)
+        if condition is None:
+            copy.wait_send()
+        else:
+            pl.when(condition)(copy.wait_send)
 
     def go(copy, condition=None):
-        started.append((copy, condition))
+        slot = slot_of[id(copy)]
+        if slot in sending:
+            sent(slot)
+        sending[slot] = (copy, condition)
         if condition is None:
             copy.start()
         else:
@@ -241,7 +254,10 @@
         )
         return Halo(*parts, buffer, pl.ds(0, 2), pl.ds(8, 2), pl.ds(2, 6))
 
-    halos = [vec_halo(k) for k in range(3)]
+    halos = []
+    for k in range(3):
+        used["send"] = 0
+        halos.append(vec_halo(k))
     coef_halo = coef_halo(lambda planes, rows: coef.at[:, planes, rows])
     loads[0].wait()
     halos[0][0].send()
@@ -454,19 +470,25 @@
     for stage, (place, slots) in enumerate(((in_plane, slots_a), (z, slots_b))):
         part[stage] = row_sum
         slots[place] = row_sum
-        copies = [remote(part.at[stage], slots.at[place], peer) for peer in peers(stage)]
-        for copy in copies:
-            go(copy)
-        for copy in copies:
-            arrive(copy)
+        send_sem, recv_sem = send_sems.at[used["send"] + stage], recv_sems.at[used["receive"] + stage]
+
+        def message(src, dst, device):
+            return pltpu.make_async_remote_copy(
+                src_ref=src, dst_ref=dst, send_sem=send_sem, recv_sem=recv_sem,
+                device_id=device, device_id_type=MESH_ID,
+            )
+
+        for peer in peers(stage):
+            message(part.at[stage], slots.at[place], peer).start()
+        rest = slots.at[pl.ds(0, slots.shape[0] - 1)]
+        all_of_them = message(rest, rest, (slab, other))
+        all_of_them.wait_recv()
+        all_of_them.wait_send()
         row_sum = jnp.sum(slots[...], axis=0)
     gram_out[...] = row_sum
 
-    for copy, condition in started:
-        if condition is None:
-            copy.wait_send()
-        else:
-            pl.when(condition)(copy.wait_send)
+    for slot in list(sending):
+        sent(slot)
 
 
 def combine_kernel(vec, w2, y1, q, gram, basis, search, hess, b_out, s_out, out_sems):
@@ -540,7 +562,7 @@
     f32 = jnp.float32
     hbm_spec = pl.BlockSpec(memory_space=pltpu.HBM)
     vmem_spec = pl.BlockSpec(memory_space=pltpu.VMEM)
-    n_remote = 14 * 3 + 5 + 2 * NX_T * NY_T + NZ_T
+    n_send, n_receive = 14 + 5 + 2, 14 * 3 + 5 + 2
     kept = (
         jax.ShapeDtypeStruct((3, 4, 16, ROWS, 256), f32),
         jax.ShapeDtypeStruct((4, 6, 16, 256), f32),
@@ -563,8 +585,8 @@
             pltpu.VMEM((2, 1, HALF), f32),
             pltpu.VMEM((2 * NX_T * NY_T, 1, HALF), f32),
             pltpu.VMEM((NZ_T, 1, HALF), f32),
-            pltpu.SemaphoreType.DMA((n_remote,)),
-            pltpu.SemaphoreType.DMA((n_remote,)),
+            pltpu.SemaphoreType.DMA((n_send,)),
+            pltpu.SemaphoreType.DMA((n_receive,)),
             pltpu.SemaphoreType.DMA((4,)),
             pltpu.SemaphoreType.REGULAR((3,)),
         ],

time: 54.3 us -> 53.2 us (0.980)
  Pallas kernels: 53.5 us -> 52.5 us
    pallas_call x1, Pallas kernels: 51.1 us -> 50.1 us  [per_device(): pl.pallas_call(krylov_kernel, out_shape=kept, in_specs=[hbm_spec] * 4, ou...]
where the time goes in v7:
time: 53.2 us; the launch traced here: 53.1 us
  Pallas kernels  52.5 us (99%)
  between operations  0.64 us (1%)
    pallas_call x1, Pallas kernels, per_device(): pl.pallas_call(krylov_kernel, out_shape=kept, in_specs=[hbm_spec] * 4, ou...  50.1 us
    pallas_call x1, Pallas kernels, per_device(): pl.pallas_call(combine_kernel, out_shape=(jax.ShapeDtypeStruct((4, 4, 6,...  2.41 us

profile of v7, /device:TPU:1, one launch (start us, length us, event | category | flops | bytes accessed | tf_op | source)
XLA Modules:
  0.0 53.1 jit_solution(13858734274778663520)
XLA Ops:
  0.6 50.1 %krylov.1 = (f32[3,4,16,24,256]{4,3,2,1,0:T(8,128)S(1)}, f32[4,6,16,256]{3,2,1,0:T(8,128)S(1)}, f32[3,3,8,24,256]{4,3,2,1,0:T(8,128)S(1)}, f32[3,12,24,256]{3,2,1,0:T(8,128)S(1)}, f32[1,128]{1,0:T(1,128)S(1)}) custom-call(f32[4,6,16,256]{3,2,1,0:T(8,128)} %start.1, f32[3,6,16,256]{3,2,1,0:T(8,128)} %wind.1, f32[6,16,256]{2,1,0:T(8,128)} %reac.1, ...), custom_call_target="tpu_custom_call" | custom-call | tf_op jit(solution)/shard_map/krylov/pallas_call | solution.py:574
  50.7 2.4 %combine.1 = (f32[4,4,6,16,256]{4,3,2,1,0:T(8,128)}, f32[3,4,6,16,256]{4,3,2,1,0:T(8,128)}, f32[4,3]{1,0:T(4,128)}) custom-call(f32[3,4,16,24,256]{4,3,2,1,0:T(8,128)S(1)} %get-tuple-element.8.vec, f32[4,6,16,256]{3,2,1,0:T(8,128)S(1)} %get-tuple-element.9.w2, f32[3,3,8,24,256]{4,3,2,1,0:T(8,128)S(1)} %get-tuple-element.10.y1, ...), custom_call_target="tpu_custom_call" | custom-call | tf_op jit(solution)/shard_map/combine/pallas_call | solution.py:598

commit v8 on v7

--- a/solution.py
+++ b/solution.py
@@ -146,7 +146,7 @@
     pl.semaphore_wait(
         barrier, count + has_left.astype(jnp.int32) + has_right.astype(jnp.int32)
     )
-    expected = tell(0)
+    expected = [tell(0)]
 
     used = {"send": 0, "receive": 0}
 
@@ -400,27 +400,68 @@
     def vectors(i, f, j):
         return vec[i, f, 5 + j, own_rows, :] if i < 3 else w2[f, j]
 
-    def dots(new, olds):
+    def dots(pairs, shift=None):
+        needed = sorted({i for pair in pairs for i in pair})
+
         def step(j, accs):
             accs = list(accs)
             for f in range(4):
-                b = vectors(new, f, j)
-                for i, old in enumerate(olds):
-                    prod = b * (b if old == new else vectors(old, f, j))
-                    accs[i] = accs[i] + (
+                raw = {}
+                for i in needed:
+                    for at in (i,) if shift is None or i == 0 else (i - 1, i):
+                        if at not in raw:
+                            raw[at] = vectors(at, f, j)
+                y = {i: raw[i] if shift is None or i == 0 else raw[i] - shift * raw[i - 1] for i in needed}
+                for n, (i, k) in enumerate(pairs):
+                    prod = y[i] * y[k]
+                    accs[n] = accs[n] + (
                         (prod[0:8, 0:HALF] + prod[0:8, HALF:]) + (prod[8:16, 0:HALF] + prod[8:16, HALF:])
                     )
             return tuple(accs)
 
         zero = jnp.zeros((8, HALF), jnp.float32)
-        return lax.fori_loop(0, 6, step, tuple(zero for _ in olds), unroll=2)
+        return lax.fori_loop(0, 6, step, tuple(zero for _ in pairs), unroll=2)
 
     def pack(total, sums, at):
         for i, s in enumerate(sums):
             total = jnp.where(lane8 == at + i, jnp.sum(s, axis=1, keepdims=True), total)
         return total
 
-    def application(k, target, after_pressure=lambda: None):
+    class Reduction:
+        def __init__(self, n):
+            self.n = n
+
+        def message(self, stage, src, dst, device):
+            at = 2 * self.n + stage
+            return pltpu.make_async_remote_copy(
+                src_ref=src, dst_ref=dst, send_sem=send_sems.at[used["send"] + at],
+                recv_sem=recv_sems.at[used["receive"] + at], device_id=device, device_id_type=MESH_ID,
+            )
+
+        def send(self, stage, row):
+            place, slots = ((in_plane, slots_a), (z, slots_b))[stage]
+            part[self.n, stage] = row
+            slots[self.n, place] = row
+            for peer in peers(stage):
+                self.message(stage, part.at[self.n, stage], slots.at[self.n, place], peer).start()
+
+        def finish(self, stage):
+            slots = (slots_a, slots_b)[stage]
+            rest = slots.at[self.n, pl.ds(0, slots.shape[1] - 1)]
+            everything = self.message(stage, rest, rest, (slab, other))
+            everything.wait_recv()
+            everything.wait_send()
+            return jnp.sum(slots[self.n], axis=0)
+
+        def whole(self, row):
+            for stage in range(2):
+                self.send(stage, row)
+                row = self.finish(stage)
+            return row
+
+    reductions = [Reduction(0), Reduction(1)]
+
+    def application(k, target, waiting, waited, after_pressure=lambda: None):
         p_halo, near, far, schur_far = halos[k]
         arrive(p_halo.to_other)
         if k == 0:
@@ -428,11 +469,13 @@
             lax.fori_loop(2, 8, prepare, 0, unroll=2)
         pressure_inner(k)
         schur_far.send()
+        kept = waiting()
         p_halo.forward()
         if k == 0:
             coef_halo.forward()
         p_halo.finish()
         near.forward()
+        waited()
         if k == 0:
             coef_halo.finish()
             for planes in (0, 8):
@@ -444,54 +487,53 @@
         far.finish()
         schur_far.finish()
         velocity_outer(k, target, after_pressure)
-
-    application(0, lambda f, j: vec.at[1, f, 5 + j], halos[1][0].send)
-    gram = jnp.zeros((8, HALF), jnp.float32)
-    at = 0
-    for k in range(2):
-        halos[k + 1][1].send()
-        halos[k + 1][2].send()
-        hear(k, expected)
-        expected = tell(k + 1)
-        if k == 0:
-            gram = pack(gram, dots(0, (0,)), 0)
-            at = 1
-        olds = tuple(range(k + 2))
-        gram = pack(gram, dots(k + 1, olds), at)
-        at += len(olds)
-        if k == 0:
-            application(1, lambda f, j: vec.at[2, f, 5 + j], halos[2][0].send)
-        else:
-            application(2, lambda f, j: w2.at[f, j])
-    hear(2, expected)
-    gram = pack(gram, dots(3, (0, 1, 2, 3)), at)
-
-    row_sum = jnp.sum(gram, axis=0, keepdims=True)
-    for stage, (place, slots) in enumerate(((in_plane, slots_a), (z, slots_b))):
-        part[stage] = row_sum
-        slots[place] = row_sum
-        send_sem, recv_sem = send_sems.at[used["send"] + stage], recv_sems.at[used["receive"] + stage]
-
-        def message(src, dst, device):
-            return pltpu.make_async_remote_copy(
-                src_ref=src, dst_ref=dst, send_sem=send_sem, recv_sem=recv_sem,
-                device_id=device, device_id_type=MESH_ID,
-            )
-
-        for peer in peers(stage):
-            message(part.at[stage], slots.at[place], peer).start()
-        rest = slots.at[pl.ds(0, slots.shape[0] - 1)]
-        all_of_them = message(rest, rest, (slab, other))
-        all_of_them.wait_recv()
-        all_of_them.wait_send()
-        row_sum = jnp.sum(slots[...], axis=0)
-    gram_out[...] = row_sum
+        return kept
+
+    def pass_on(turn):
+        hear(turn, expected[turn])
+        expected.append(tell(turn + 1))
+
+    def shift_known():
+        row = reductions[0].finish(1)
+
+        def entry(i):
+            return jnp.sum(jnp.where(lane_row == i, row, 0.0), axis=1, keepdims=True)
+
+        c = jnp.broadcast_to(entry(1) / entry(0), (1, HALF))
+        c = jnp.concatenate([c, c], axis=1)
+        pairs = ((0, 0), (1, 0), (1, 1), (2, 0), (2, 1), (2, 2))
+        return c, pack(jnp.zeros((8, HALF), jnp.float32), dots(pairs, c), 0)
+
+    def nothing():
+        return None
+
+    lane_row = lax.broadcasted_iota(jnp.int32, (1, HALF), 1)
+    application(
+        0, lambda f, j: vec.at[1, f, 5 + j], lambda: pass_on(0), lambda: pass_on(1), halos[1][0].send
+    )
+    halos[1][1].send()
+    halos[1][2].send()
+    hear(2, expected[2])
+    opening = pack(jnp.zeros((8, HALF), jnp.float32), dots(((0, 0), (1, 0))), 0)
+    reductions[0].send(0, jnp.sum(opening, axis=0, keepdims=True))
+    application(
+        1, lambda f, j: vec.at[2, f, 5 + j], nothing,
+        lambda: reductions[0].send(1, reductions[0].finish(0)), halos[2][0].send,
+    )
+    halos[2][1].send()
+    halos[2][2].send()
+    shift, gram = application(2, lambda f, j: w2.at[f, j], shift_known, nothing)
+    gram = pack(gram, dots(((3, 0), (3, 1), (3, 2), (3, 3)), shift), 6)
+
+    total = reductions[1].whole(jnp.sum(gram, axis=0, keepdims=True))
+    lane1 = lax.broadcasted_iota(jnp.int32, (1, HALF), 1)
+    gram_out[...] = jnp.where(lane1 == 10, shift[:, 0:HALF], total)
 
     for slot in list(sending):
         sent(slot)
 
 
-def combine_kernel(vec, w2, y1, q, gram, basis, search, hess, b_out, s_out, out_sems):
+def combine_kernel(vec, w2, y1, q, gram, basis, search, hess, b_out, s_out, h_out, out_sems):
     own_rows = pl.ds(pl.multiple_of(8 * lax.axis_index("sub"), 8), 16)
 
     total = gram[...]
@@ -512,10 +554,13 @@
                 inverse[i] = 1.0 / low[i, i]
             else:
                 low[i, j] = value * inverse[j]
+    shift = entry(10)
     h = {}
     for j in range(3):
         for i in range(j + 2):
             value = low[j + 1, i]
+            if j == 0 and i == 0:
+                value = value + shift * low[0, 0]
             for m in range(j):
                 if i <= m + 1:
                     value = value - low[j, m] * h[i, m]
@@ -525,21 +570,24 @@
     table = jnp.zeros((4, HALF), jnp.float32)
     for (i, j), value in h.items():
         table = jnp.where(jnp.logical_and(at_row == i, at_col == j), value, table)
-    hess[...] = table[:, 0:3]
+    h_out[...] = table[:, 0:3]
+    writes = [pltpu.make_async_copy(h_out, hess, out_sems.at[4, 0])]
+    writes[0].start()
 
     def wide(v):
         return jnp.concatenate([v, v], axis=1)
 
     scale = {key: wide(v) for key, v in low.items()}
     inv = {key: wide(v) for key, v in inverse.items()}
-
-    writes = []
+    c = wide(shift)
+
     for f in range(4):
 
         def body(j, _):
             raw = [vec[i, f, 5 + j, own_rows, :] for i in range(3)] + [w2[f, j]]
             found = [y1[i, f, 1 + j, own_rows, :] if f < 3 else q[i, 3 + j, own_rows, :] for i in range(3)]
             for values, dst in ((raw, b_out), (found, s_out)):
+                values = values[:1] + [b - c * a for a, b in zip(values, values[1:])]
                 done = []
                 for i, value in enumerate(values):
                     for m in range(i):
@@ -562,7 +610,7 @@
     f32 = jnp.float32
     hbm_spec = pl.BlockSpec(memory_space=pltpu.HBM)
     vmem_spec = pl.BlockSpec(memory_space=pltpu.VMEM)
-    n_send, n_receive = 14 + 5 + 2, 14 * 3 + 5 + 2
+    n_send, n_receive = 14 + 5 + 4, 14 * 3 + 5 + 4
     kept = (
         jax.ShapeDtypeStruct((3, 4, 16, ROWS, 256), f32),
         jax.ShapeDtypeStruct((4, 6, 16, 256), f32),
@@ -582,9 +630,9 @@
             pltpu.VMEM((16, ROWS, 256), f32),
             pltpu.VMEM((3, 10, ROWS, 256), f32),
             pltpu.VMEM((3, 10, ROWS, 256), f32),
-            pltpu.VMEM((2, 1, HALF), f32),
-            pltpu.VMEM((2 * NX_T * NY_T, 1, HALF), f32),
-            pltpu.VMEM((NZ_T, 1, HALF), f32),
+            pltpu.VMEM((2, 2, 1, HALF), f32),
+            pltpu.VMEM((2, 2 * NX_T * NY_T, 1, HALF), f32),
+            pltpu.VMEM((2, NZ_T, 1, HALF), f32),
             pltpu.SemaphoreType.DMA((n_send,)),
             pltpu.SemaphoreType.DMA((n_receive,)),
             pltpu.SemaphoreType.DMA((4,)),
@@ -603,11 +651,12 @@
             jax.ShapeDtypeStruct((4, 3), f32),
         ),
         in_specs=[vmem_spec] * 5,
-        out_specs=(hbm_spec, hbm_spec, vmem_spec),
+        out_specs=(hbm_spec, hbm_spec, hbm_spec),
         scratch_shapes=[
             pltpu.VMEM((4, 4, 6, 16, 256), f32),
             pltpu.VMEM((3, 4, 6, 16, 256), f32),
-            pltpu.SemaphoreType.DMA((4, 2)),
+            pltpu.VMEM((4, 3), f32),
+            pltpu.SemaphoreType.DMA((5, 2)),
         ],
         compiler_params=pltpu.CompilerParams(vmem_limit_bytes=24 * 2**20),
         name="combine",

time: 53.2 us -> 53 us (level)
    pallas_call x1, Pallas kernels: 2.41 us -> 1.87 us  [per_device(): pl.pallas_call(combine_kernel, out_shape=(jax.ShapeDtypeStruct((4, 4, 6,...]
where the time goes in v8:
time: 53 us; the launch traced here: 52.9 us
  Pallas kernels  52.2 us (98%)
  between operations  0.64 us (1%)
    pallas_call x1, Pallas kernels, per_device(): pl.pallas_call(krylov_kernel, out_shape=kept, in_specs=[hbm_spec] * 4, ou...  50.4 us
    pallas_call x1, Pallas kernels, per_device(): pl.pallas_call(combine_kernel, out_shape=(jax.ShapeDtypeStruct((4, 4, 6,...  1.87 us

profile of v8, /device:TPU:1, one launch (start us, length us, event | category | flops | bytes accessed | tf_op | source)
XLA Modules:
  0.0 52.9 jit_solution(3704591986585241970)
XLA Ops:
  0.6 50.4 %krylov.1 = (f32[3,4,16,24,256]{4,3,2,1,0:T(8,128)S(1)}, f32[4,6,16,256]{3,2,1,0:T(8,128)S(1)}, f32[3,3,8,24,256]{4,3,2,1,0:T(8,128)S(1)}, f32[3,12,24,256]{3,2,1,0:T(8,128)S(1)}, f32[1,128]{1,0:T(1,128)S(1)}) custom-call(f32[4,6,16,256]{3,2,1,0:T(8,128)} %start.1, f32[3,6,16,256]{3,2,1,0:T(8,128)} %wind.1, f32[6,16,256]{2,1,0:T(8,128)} %reac.1, ...), custom_call_target="tpu_custom_call" | custom-call | tf_op jit(solution)/shard_map/krylov/pallas_call | solution.py:622
  51.0 1.9 %combine.1 = (f32[4,4,6,16,256]{4,3,2,1,0:T(8,128)}, f32[3,4,6,16,256]{4,3,2,1,0:T(8,128)}, f32[4,3]{1,0:T(4,128)}) custom-call(f32[3,4,16,24,256]{4,3,2,1,0:T(8,128)S(1)} %get-tuple-element.8.vec, f32[4,6,16,256]{3,2,1,0:T(8,128)S(1)} %get-tuple-element.9.w2, f32[3,3,8,24,256]{4,3,2,1,0:T(8,128)S(1)} %get-tuple-element.10.y1, ...), custom_call_target="tpu_custom_call" | custom-call | tf_op jit(solution)/shard_map/combine/pallas_call | solution.py:646

commit v9 on v8

--- a/solution.py
+++ b/solution.py
@@ -335,8 +335,8 @@
         loop(2, functools.partial(schur, k), lambda i: i + 7, 2)
 
     def pressure_outer(k):
-        loop(8, functools.partial(guess, k), lambda i: i + 2 + 4 * lax.div(i, 4), 4)
-        loop(8, functools.partial(schur, k), lambda i: i + 3 + 2 * lax.div(i, 4), 4)
+        loop(8, functools.partial(guess, k), lambda i: i + 2 + 4 * lax.div(i, 4), 8)
+        loop(8, functools.partial(schur, k), lambda i: i + 3 + 2 * lax.div(i, 4), 8)
 
     def first_guess(k, j):
         slope = gradient(get(q, k, j), get(q, k, j + 1), get(q, k, j + 2))
@@ -356,8 +356,8 @@
             put(y1, [a + (b - c) * i for a, b, c, i in zip(f, r, value, inverse)], k, d, j)
 
     def velocity_inner(k):
-        loop(8, functools.partial(first_guess, k), lambda i: i + 1, 4)
-        loop(6, functools.partial(second_guess, k), lambda i: i + 1, 3)
+        loop(8, functools.partial(first_guess, k), lambda i: i + 1, 8)
+        loop(6, functools.partial(second_guess, k), lambda i: i + 1, 6)
 
     def velocity_outer(k, target, after_pressure=lambda: None):
         loop(2, functools.partial(first_guess, k), lambda i: 9 * i, 2)
@@ -393,7 +393,7 @@
                 store(d, j, [a + b for a, b in zip(value, slope[d])])
             return 0
 
-        lax.fori_loop(0, 6, image_velocity, 0, unroll=3)
+        lax.fori_loop(0, 6, image_velocity, 0, unroll=6)
 
     lane8 = lax.broadcasted_iota(jnp.int32, (8, HALF), 1)
 

time: 53 us -> 52 us (0.981)
  Pallas kernels: 52.2 us -> 51.3 us
    pallas_call x1, Pallas kernels: 50.4 us -> 49.4 us  [per_device(): pl.pallas_call(krylov_kernel, out_shape=kept, in_specs=[hbm_spec] * 4, ou...]
where the time goes in v9:
time: 52 us; the launch traced here: 51.9 us
  Pallas kernels  51.3 us (99%)
  between operations  0.64 us (1%)
    pallas_call x1, Pallas kernels, per_device(): pl.pallas_call(krylov_kernel, out_shape=kept, in_specs=[hbm_spec] * 4, ou...  49.4 us
    pallas_call x1, Pallas kernels, per_device(): pl.pallas_call(combine_kernel, out_shape=(jax.ShapeDtypeStruct((4, 4, 6,...  1.87 us

profile of v9, /device:TPU:1, one launch (start us, length us, event | category | flops | bytes accessed | tf_op | source)
XLA Modules:
  0.0 51.9 jit_solution(13502044896209452867)
XLA Ops:
  0.6 49.4 %krylov.1 = (f32[3,4,16,24,256]{4,3,2,1,0:T(8,128)S(1)}, f32[4,6,16,256]{3,2,1,0:T(8,128)S(1)}, f32[3,3,8,24,256]{4,3,2,1,0:T(8,128)S(1)}, f32[3,12,24,256]{3,2,1,0:T(8,128)S(1)}, f32[1,128]{1,0:T(1,128)S(1)}) custom-call(f32[4,6,16,256]{3,2,1,0:T(8,128)} %start.1, f32[3,6,16,256]{3,2,1,0:T(8,128)} %wind.1, f32[6,16,256]{2,1,0:T(8,128)} %reac.1, ...), custom_call_target="tpu_custom_call" | custom-call | tf_op jit(solution)/shard_map/krylov/pallas_call | solution.py:622
  50.0 1.9 %combine.1 = (f32[4,4,6,16,256]{4,3,2,1,0:T(8,128)}, f32[3,4,6,16,256]{4,3,2,1,0:T(8,128)}, f32[4,3]{1,0:T(4,128)}) custom-call(f32[3,4,16,24,256]{4,3,2,1,0:T(8,128)S(1)} %get-tuple-element.8.vec, f32[4,6,16,256]{3,2,1,0:T(8,128)S(1)} %get-tuple-element.9.w2, f32[3,3,8,24,256]{4,3,2,1,0:T(8,128)S(1)} %get-tuple-element.10.y1, ...), custom_call_target="tpu_custom_call" | custom-call | tf_op jit(solution)/shard_map/combine/pallas_call | solution.py:646

commit v10 on v9

--- a/solution.py
+++ b/solution.py
@@ -420,7 +420,7 @@
             return tuple(accs)
 
         zero = jnp.zeros((8, HALF), jnp.float32)
-        return lax.fori_loop(0, 6, step, tuple(zero for _ in pairs), unroll=2)
+        return lax.fori_loop(0, 6, step, tuple(zero for _ in pairs), unroll=6)
 
     def pack(total, sums, at):
         for i, s in enumerate(sums):
@@ -466,7 +466,7 @@
         arrive(p_halo.to_other)
         if k == 0:
             arrive(coef_halo.to_other)
-            lax.fori_loop(2, 8, prepare, 0, unroll=2)
+            lax.fori_loop(2, 8, prepare, 0, unroll=6)
         pressure_inner(k)
         schur_far.send()
         kept = waiting()

time: 52 us -> 52 us (level)
  no operation moved by 1% of the time
where the time goes in v10:
time: 52 us; the launch traced here: 51.9 us
  Pallas kernels  51.3 us (99%)
  between operations  0.64 us (1%)
    pallas_call x1, Pallas kernels, per_device(): pl.pallas_call(krylov_kernel, out_shape=kept, in_specs=[hbm_spec] * 4, ou...  49.4 us
    pallas_call x1, Pallas kernels, per_device(): pl.pallas_call(combine_kernel, out_shape=(jax.ShapeDtypeStruct((4, 4, 6,...  1.87 us

profile of v10, /device:TPU:1, one launch (start us, length us, event | category | flops | bytes accessed | tf_op | source)
XLA Modules:
  0.0 51.9 jit_solution(10839650818839356127)
XLA Ops:
  0.6 49.4 %krylov.1 = (f32[3,4,16,24,256]{4,3,2,1,0:T(8,128)S(1)}, f32[4,6,16,256]{3,2,1,0:T(8,128)S(1)}, f32[3,3,8,24,256]{4,3,2,1,0:T(8,128)S(1)}, f32[3,12,24,256]{3,2,1,0:T(8,128)S(1)}, f32[1,128]{1,0:T(1,128)S(1)}) custom-call(f32[4,6,16,256]{3,2,1,0:T(8,128)} %start.1, f32[3,6,16,256]{3,2,1,0:T(8,128)} %wind.1, f32[6,16,256]{2,1,0:T(8,128)} %reac.1, ...), custom_call_target="tpu_custom_call" | custom-call | tf_op jit(solution)/shard_map/krylov/pallas_call | solution.py:622
  50.1 1.9 %combine.1 = (f32[4,4,6,16,256]{4,3,2,1,0:T(8,128)}, f32[3,4,6,16,256]{4,3,2,1,0:T(8,128)}, f32[4,3]{1,0:T(4,128)}) custom-call(f32[3,4,16,24,256]{4,3,2,1,0:T(8,128)S(1)} %get-tuple-element.8.vec, f32[4,6,16,256]{3,2,1,0:T(8,128)S(1)} %get-tuple-element.9.w2, f32[3,3,8,24,256]{4,3,2,1,0:T(8,128)S(1)} %get-tuple-element.10.y1, ...), custom_call_target="tpu_custom_call" | custom-call | tf_op jit(solution)/shard_map/combine/pallas_call | solution.py:646
